TPU v7x, 256 devices: a 8x8x2 block of a 8x8x16 slice. The times are simulated.
256 devices in a mesh: beam: 2 (over z), tm: 128 (over x, y, core).
Axes of the slice: x: 8, y: 8, z: 2, core: 2. Of those that a mesh axis runs over, the one named last changes fastest.
The devices are a block of a 8x8x16 slice.
Arguments:
- voltage: bfloat16 [2, 2, 16777216], P(None, None, ('beam', 'tm')), parts along dimension 2, may hold values from -11 to 11
- delays: int32 [64, 2048], replicated, may hold values from 0 to 96, as said below
- chan_mask: int32 [4096], P('beam'), parts along dimension 0, may hold values 0 or 1
Outputs:
- zscore: float32 [64, 8192], P(None, ('beam', 'tm')), parts along dimension 1
- trial_stats: float32 [3, 128], P(None, 'beam'), parts along dimension 1
There are 2 independent parts, one for each index of `beam`. A program takes and returns all parts, laid end to end along the dimension named above; an argument that names none is the same for every part. Nothing has to cross between parts.
Inputs may be any that keep to these rules, and one draw needn't show every extreme that they name: For each trial the delays never rise from one channel to the next; the last channel's delays are 0, and the first channel's delay of some trial is 96.
All inputs are finite; a program needn't handle non-finite values.
Results may differ from a plain program's by a relative error of at most 0.002.
Values may be sent and summed in bfloat16 or wider, within the bound.
A program may use at most 64 MiB of HBM per device.

v0:
```python
import math

import jax
import jax.numpy as jnp
from jax import lax
from jax.sharding import Mesh
from jax.sharding import PartitionSpec as P

NCHAN = 2048
TAPS = 16
DSPAN = 3
TM = ("tm_0", "tm_1", "tm_2")
BEAM_TM = ("beam", "tm_0", "tm_1", "tm_2")


highest = lax.Precision.HIGHEST
shift_group = 8


def passed_along(value, axis, steps):
    count = lax.axis_size(axis)
    first, last = (max(0, -steps), min(count, count - steps))
    return lax.ppermute(value, axis, [(source, source + steps) for source in range(first, last)])


def all_in_one(shard, axis):
    leaves = jax.tree.leaves(shard)
    sequence = sorted(range(len(leaves)), key=lambda k: -leaves[k].size)
    width = (1, *leaves[sequence[0]].shape)[-1]
    lines = [
        jnp.pad(leaves[k].reshape(-1), (0, -leaves[k].size % width)).reshape(-1, width)
        for k in sequence
    ]
    both, at, found = (lax.all_gather(jnp.concatenate(lines), axis), 0, {})
    for k, line in zip(sequence, lines):
        slab = both[:, at : at + len(line)].reshape(len(both), -1)
        found[k] = slab[:, : leaves[k].size].reshape(-1, *leaves[k].shape)
        at += len(line)
    numbers = iter(range(len(leaves)))
    return jax.tree.map(lambda _: found[next(numbers)], shard)


def merged_by_axis(shard, axes, combine):
    for axis in axes:
        pieces = all_in_one(shard, axis)
        shard = jax.tree.map(lambda part: part[0], pieces)
        for k in range(1, lax.axis_size(axis)):
            shard = combine(shard, jax.tree.map(lambda part: part[k], pieces))
    return shard


def prototype(tap_count, chan_count):
    length = tap_count * chan_count
    position = jnp.arange(length, dtype=jnp.float32)
    centred = (position - (length - 1) / 2.0) / chan_count
    window = 0.54 - 0.46 * jnp.cos(2.0 * jnp.pi * position / (length - 1))
    shaped = jnp.sinc(centred) * window
    shaped = shaped * jnp.sqrt(chan_count / jnp.sum(shaped * shaped))
    return shaped.reshape(tap_count, chan_count)


def phase_table(row_count, col_count, period):
    product = (
        jnp.arange(row_count, dtype=jnp.int32)[:, None]
        * jnp.arange(col_count, dtype=jnp.int32)[None, :]
        % period
    )
    angles = product.astype(jnp.float32) * (-2.0 * jnp.pi / period)
    return (jnp.cos(angles), jnp.sin(angles))


def spectral_power(weighted, chan_count):
    frame_count = weighted.shape[2]
    low_count = chan_count // 128
    split_up = weighted.reshape(2, 2, frame_count, low_count, 128)
    real_part = split_up[:, 0]
    imag_part = split_up[:, 1]
    cos_first, sin_first = phase_table(low_count, low_count, low_count)
    section_real = jnp.einsum(
        "pfmn,mk->pfkn", real_part, cos_first, precision=highest
    ) - jnp.einsum("pfmn,mk->pfkn", imag_part, sin_first, precision=highest)
    section_imag = jnp.einsum(
        "pfmn,mk->pfkn", real_part, sin_first, precision=highest
    ) + jnp.einsum("pfmn,mk->pfkn", imag_part, cos_first, precision=highest)
    cos_twist, sin_twist = phase_table(low_count, 128, chan_count)
    twist_real = section_real * cos_twist - section_imag * sin_twist
    twist_imag = section_real * sin_twist + section_imag * cos_twist
    cos_second, sin_second = phase_table(128, 128, 128)
    scale_factor = 1.0 / math.sqrt(chan_count)
    cos_second = cos_second * scale_factor
    sin_second = sin_second * scale_factor
    final_real = jnp.einsum(
        "pfkn,nj->pfkj", twist_real, cos_second, precision=highest
    ) - jnp.einsum("pfkn,nj->pfkj", twist_imag, sin_second, precision=highest)
    final_imag = jnp.einsum(
        "pfkn,nj->pfkj", twist_real, sin_second, precision=highest
    ) + jnp.einsum("pfkn,nj->pfkj", twist_imag, cos_second, precision=highest)
    energy = jnp.sum(final_real * final_real + final_imag * final_imag, axis=0)
    return jnp.transpose(energy, (2, 1, 0)).reshape(chan_count, frame_count).astype(jnp.bfloat16)


def dedisperse(padded, delays, out_width, max_delay):
    chan_count = padded.shape[0]
    group_count = (max_delay + shift_group) // shift_group
    needed = out_width + group_count * shift_group
    padded = jnp.concatenate(
        [padded, jnp.zeros((chan_count, needed - padded.shape[1]), padded.dtype)], axis=1
    )
    within = jnp.arange(shift_group, dtype=jnp.int32)

    def add_group(group_index, running):
        base = (group_index * shift_group).astype(jnp.int32)
        window = lax.dynamic_slice_in_dim(padded, base, out_width + shift_group - 1, 1)
        stacked = jnp.stack(
            [window[:, offset : offset + out_width] for offset in range(shift_group)]
        )
        targets = base + within
        selector = (delays[:, None, :] == targets[None, :, None]).astype(jnp.bfloat16)
        return running + jnp.einsum(
            "dsk,skt->dt", selector, stacked, preferred_element_type=jnp.float32
        )

    zero_sums = jnp.zeros((delays.shape[0], out_width), jnp.float32)
    return lax.fori_loop(0, group_count, add_group, zero_sums)


def combine_moments(left_side, right_side):
    count_left, mean_left, second_left, peak_left = left_side
    count_right, mean_right, second_right, peak_right = right_side
    count_both = count_left + count_right
    mean_shift = mean_right - mean_left
    mean_both = mean_left + mean_shift * (count_right / count_both)
    second_both = (
        second_left
        + second_right
        + mean_shift * mean_shift * (count_left * count_right / count_both)
    )
    return (count_both, mean_both, second_both, jnp.maximum(peak_left, peak_right))


def per_device(voltage, delays, chan_mask):
    frame_count = voltage.shape[2] // NCHAN
    framed = voltage.reshape(2, 2, frame_count, NCHAN)
    history = passed_along(framed[:, :, frame_count - (TAPS - 1) :], TM, 1)
    extended = jnp.concatenate([history, framed], axis=2)
    coeffs = prototype(TAPS, NCHAN)
    weighted = jnp.zeros((2, 2, frame_count, NCHAN), jnp.float32)
    for tap_index in range(TAPS):
        weighted = weighted + coeffs[tap_index] * extended[
            :, :, tap_index : tap_index + frame_count
        ].astype(jnp.float32)
    detected = spectral_power(weighted, NCHAN)
    masked = detected * chan_mask.astype(jnp.bfloat16)[:, None]
    max_delay = DSPAN * frame_count
    gathered = masked
    held_shards = 1
    while held_shards < DSPAN + 1:
        fetched = passed_along(gathered, TM, -held_shards)
        gathered = jnp.concatenate([gathered, fetched], axis=1)
        held_shards = held_shards * 2
    series = dedisperse(gathered, delays, frame_count, max_delay)
    local_frames = series.shape[1]
    local_mean = jnp.sum(series, axis=1) / local_frames
    local_dev = series - local_mean[:, None]
    counts = jnp.full(local_mean.shape, float(local_frames), jnp.float32)
    merged = merged_by_axis(
        (counts, local_mean, jnp.sum(local_dev * local_dev, axis=1), jnp.max(series, axis=1)),
        TM,
        combine_moments,
    )
    count_all, average, second_all, peak_value = merged
    variance = second_all / count_all
    centred = series - average[:, None]
    deviation = jnp.sqrt(variance + 1e-05)
    zscore = centred / deviation[:, None]
    live_count = jnp.maximum(jnp.sum(chan_mask).astype(jnp.float32), 1.0)
    trial_stats = jnp.stack(
        [average / live_count, deviation / live_count, (peak_value - average) / deviation]
    )
    return (zscore, trial_stats)


def solution(mesh):
    split = Mesh(
        mesh.devices.reshape(mesh.shape["beam"], 8, 8, 2), ("beam", "tm_0", "tm_1", "tm_2")
    )
    return jax.shard_map(
        per_device,
        mesh=split,
        in_specs=(P(None, None, BEAM_TM), P(), P("beam")),
        out_specs=(P(None, BEAM_TM), P(None, "beam")),
        check_vma=False,
    )
```

profile of v0, /device:TPU:513, one launch (start us, length us, event | category | flops | bytes accessed | tf_op | source)
XLA Modules:
  0.0 123.3 jit_solution(1762321827538677849)
XLA Ops:
  0.6 1.4 %reshape.1935 = bf16[2,2,32,2048]{3,2,1,0:T(8,128)(2,1)S(1)} reshape(bf16[2,2,65536]{2,1,0:T(2,128)(2,1)} %param.5) | data formatting | bytes 1048576 | tf_op jit(solution)/shard_map/reshape | solution.py:143
  2.2 5.7 %collective-permute-start = (bf16[2,2,15,2048]{3,2,0,1:T(8,128)(2,1)S(1)}, bf16[2,2,15,2048]{3,2,0,1:T(8,128)(2,1)S(1)}, u32[]{:S(2)}, u32[]{:S(2)}) collective-permute-start(bf16[2,2,15,2048]{3,2,0,1:T(8,128)(2,1)S(1)} %slice.661), channel_id=1, source_target_pairs={{0,1},{1,2},{2,3},{3,4},{4,5},{5,6},{6,7},{7,8},{8,9},{9,10},{10,1... | collective-permute-start | bytes 737288 | tf_op jit(solution)/shard_map/ppermute | solution.py:23
  7.9 1.2 %multiply_reduce_fusion = f32[]{:T(128)} fusion(), kind=kLoop, calls=%fused_computation.128 | loop fusion | flops 1343487 | bytes 4 | tf_op jit(solution)/shard_map/reduce_sum | solution.py:58
  11.3 13.6 %collective-permute-done = bf16[2,2,15,2048]{3,2,0,1:T(8,128)(2,1)S(1)} collective-permute-done((bf16[2,2,15,2048]{3,2,0,1:T(8,128)(2,1)S(1)}, bf16[2,2,15,2048]{3,2,0,1:T(8,128)(2,1)S(1)}, u32[]{:S(2)}, u32[]{:S(2)}) %collective-permute-start) | collective-permute-done | bytes 245792 | tf_op jit(solution)/shard_map/ppermute | solution.py:23
  24.9 2.6 %multiply_add_fusion = f32[2,2,32,2048]{3,2,0,1:T(8,128)S(1)} fusion(bf16[2,2,32,2048]{3,2,0,1:T(8,128)(2,1)S(1)} %copy.12, bf16[2,2,15,2048]{3,2,0,1:T(8,128)(2,1)S(1)} %collective-permute-done, f32[2048]{0:T(1024)S(1)} %get-tuple-element.149, f32[2048]{0:T(1024)S(1)} %get-tuple-element.150, f32[2048]{0:T(1024)S(1)} %get-tuple-element.151, ...), kind=kLoop, calls=%fused_computation.61 | loop fusion | flops 24117248 | bytes 1949696 | tf_op jit(solution)/shard_map/add | solution.py:149
  34.3 4.3 %collective-permute-start.1 = (bf16[2048,32]{1,0:T(8,128)(2,1)S(1)}, bf16[2048,32]{1,0:T(8,128)(2,1)S(1)}, u32[]{:S(2)}, u32[]{:S(2)}) collective-permute-start(bf16[2048,32]{1,0:T(8,128)(2,1)S(1)} %bitcast_multiply_fusion), channel_id=1, source_target_pairs={{1,0},{2,1},{3,2},{4,3},{5,4},{6,5},{7,6},{8,7},{9,8},{10,9},{11,1... | collective-permute-start | bytes 393224 | tf_op jit(solution)/shard_map/ppermute | solution.py:23
  38.7 6.2 %collective-permute-done.1 = bf16[2048,32]{1,0:T(8,128)(2,1)S(1)} collective-permute-done((bf16[2048,32]{1,0:T(8,128)(2,1)S(1)}, bf16[2048,32]{1,0:T(8,128)(2,1)S(1)}, u32[]{:S(2)}, u32[]{:S(2)}) %collective-permute-start.1) | collective-permute-done | bytes 131104 | tf_op jit(solution)/shard_map/ppermute | solution.py:23
  45.1 1.5 %collective-permute-start.2 = (bf16[2048,64]{1,0:T(8,128)(2,1)S(1)}, bf16[2048,64]{1,0:T(8,128)(2,1)S(1)}, u32[]{:S(2)}, u32[]{:S(2)}) collective-permute-start(bf16[2048,64]{1,0:T(8,128)(2,1)S(1)} %pad_maximum_fusion.1), channel_id=1, source_target_pairs={{2,0},{3,1},{4,2},{5,3},{6,4},{7,5},{8,6},{9,7},{10,8},{11,9},{12,... | collective-permute-start | bytes 786440 | tf_op jit(solution)/shard_map/ppermute | solution.py:23
  47.3 12.1 %collective-permute-done.2 = bf16[2048,64]{1,0:T(8,128)(2,1)S(1)} collective-permute-done((bf16[2048,64]{1,0:T(8,128)(2,1)S(1)}, bf16[2048,64]{1,0:T(8,128)(2,1)S(1)}, u32[]{:S(2)}, u32[]{:S(2)}) %collective-permute-start.2) | collective-permute-done | bytes 262176 | tf_op jit(solution)/shard_map/ppermute | solution.py:23
  59.4 0.9 maximum_maximum_fusion
  61.4 17.2 %while.14 = (s32[]{:T(128)}, f32[64,32]{0,1:T(8,128)S(1)}, s32[64,2048]{1,0:T(8,128)S(1)}, bf16[2048,136]{0,1:T(8,128)(2,1)S(1)}, s32[]{:T(128)}, /*index=5*/s32...) while((s32[]{:T(128)}, f32[64,32]{0,1:T(8,128)S(1)}, ...), condition=%wide.region_3.4_spmd.clone, body=%wide.region_2.3_spmd.clone.sunk | while | flops 68161560 | bytes 3686781 | solution.py:124
  61.8 0.9 fusion.252
  63.1 0.9 fusion.252
  64.4 0.9 fusion.252
  65.8 0.9 fusion.252
  67.1 0.9 fusion.252
  68.4 0.9 fusion.252
  71.1 0.9 fusion.252
  72.4 0.9 fusion.252
  75.1 0.9 fusion.252
  76.4 0.9 fusion.252
  78.8 15.6 %all-gather.3 = f32[8,4,64]{2,1,0:T(4,128)S(1)} all-gather(f32[1,4,64]{2,1,0:T(4,128)S(1)} %maximum_bitcast_fusion), channel_id=2, replica_groups=mesh['beam'=2,'tm_0'=8,'tm_1'=8,'tm_2'=2] {'tm_0'}, dimensions={0}, use_global_device_ids=true | all-gather | bytes 9216 | tf_op jit(solution)/shard_map/all_gather | solution.py:34
  94.4 16.1 %all-gather.4 = f32[8,4,64]{2,1,0:T(4,128)S(1)} all-gather(f32[1,4,64]{2,1,0:T(4,128)S(1)} %maximum_bitcast_fusion.1), channel_id=3, replica_groups=mesh['beam'=2,'tm_0'=8,'tm_1'=8,'tm_2'=2] {'tm_1'}, dimensions={0}, use_global_device_ids=true | all-gather | bytes 9216 | tf_op jit(solution)/shard_map/all_gather | solution.py:34
  110.7 11.4 %all-gather.5 = f32[2,4,64]{2,1,0:T(4,128)S(1)} all-gather(f32[1,4,64]{2,1,0:T(4,128)S(1)} %maximum_bitcast_fusion.2), channel_id=4, replica_groups=mesh['beam'=2,'tm_0'=8,'tm_1'=8,'tm_2'=2] {'tm_2'}, dimensions={0}, use_global_device_ids=true | all-gather | bytes 3072 | tf_op jit(solution)/shard_map/all_gather | solution.py:34
  (164 shorter events, 17.8 us)
Async XLA Ops:
  2.0 8.5 %copy-start = (s32[2048]{0:T(1024)S(1)}, s32[2048]{0:T(1024)}, u32[]{:S(2)}) copy-start(s32[2048]{0:T(1024)} %param.7) | copy-start | bytes 24580
  2.2 22.7 %collective-permute-start = (bf16[2,2,15,2048]{3,2,0,1:T(8,128)(2,1)S(1)}, bf16[2,2,15,2048]{3,2,0,1:T(8,128)(2,1)S(1)}, u32[]{:S(2)}, u32[]{:S(2)}) collective-permute-start(bf16[2,2,15,2048]{3,2,0,1:T(8,128)(2,1)S(1)} %slice.661), channel_id=1, source_target_pairs={{0,1},{1,2},{2,3},{3,4},{4,5},{5,6},{6,7},{7,8},{8,9},{9,10},{10,1... | collective-permute-start | bytes 737288 | tf_op jit(solution)/shard_map/ppermute | solution.py:23
  34.3 10.5 %collective-permute-start.1 = (bf16[2048,32]{1,0:T(8,128)(2,1)S(1)}, bf16[2048,32]{1,0:T(8,128)(2,1)S(1)}, u32[]{:S(2)}, u32[]{:S(2)}) collective-permute-start(bf16[2048,32]{1,0:T(8,128)(2,1)S(1)} %bitcast_multiply_fusion), channel_id=1, source_target_pairs={{1,0},{2,1},{3,2},{4,3},{5,4},{6,5},{7,6},{8,7},{9,8},{10,9},{11,1... | collective-permute-start | bytes 393224 | tf_op jit(solution)/shard_map/ppermute | solution.py:23
  45.1 14.3 %collective-permute-start.2 = (bf16[2048,64]{1,0:T(8,128)(2,1)S(1)}, bf16[2048,64]{1,0:T(8,128)(2,1)S(1)}, u32[]{:S(2)}, u32[]{:S(2)}) collective-permute-start(bf16[2048,64]{1,0:T(8,128)(2,1)S(1)} %pad_maximum_fusion.1), channel_id=1, source_target_pairs={{2,0},{3,1},{4,2},{5,3},{6,4},{7,5},{8,6},{9,7},{10,8},{11,9},{12,... | collective-permute-start | bytes 786440 | tf_op jit(solution)/shard_map/ppermute | solution.py:23
  60.3 1.0 copy-start.1
where the time goes:
time: 124 us; the launch traced here: 123 us
  blocking collectives  43.1 us (35%)
  waiting for transfers between devices  31.9 us (26%)
  matrix products  17.3 us (14%)
  starting transfers between devices  11.6 us (9%)
  other arithmetic  8.32 us (7%)
  local copies, waits for them, and re-layouts  7.22 us (6%)
  between operations  2.27 us (2%)
  loops' own time  1.66 us (1%)
    all_gather x3, blocking collectives, all_in_one(): both, at, found = (lax.all_gather(jnp.concatenate(lines), axis), 0, {})  43.1 us
    ppermute x3, waiting for transfers between devices, passed_along(): lax.ppermute(value, axis, [(source, source + steps) for source in range(f...  31.9 us
    ppermute x3, starting transfers between devices, passed_along(): lax.ppermute(value, axis, [(source, source + steps) for source in range(f...  11.6 us
    dot_general x13, matrix products, add_group(): jnp.einsum('dsk,skt->dt', selector, stacked, preferred_element_type=jnp.f...  11.5 us
    while x91, local copies, waits for them, and re-layouts  3.45 us
    add x1, other arithmetic, per_device(): weighted + coeffs[tap_index] * extended[:, :, tap_index:tap_index + frame...  2.59 us
  transfers between devices with their start and end apart: 3, of which 3 were waited for; matrix products, arithmetic and copies ran while one was open for 2% of the time, Pallas kernels for 0%

commit v1 on v0

v1 whole, which is shorter than its diff:
```python
import functools

import jax
import jax.numpy as jnp
import numpy as np
from jax import lax
from jax.experimental import pallas as pl
from jax.experimental.pallas import tpu as pltpu
from jax.sharding import PartitionSpec as P

NCHAN = 2048
TAPS = 16
LOW = 16
HIGH = 128
BLOCK = 8
GROUP = 16
LANES = 128
DSPAN = 3
MESH = pl.DeviceIdType.MESH
F32 = jnp.float32
BF16 = jnp.bfloat16


def filter_table():
    length = TAPS * NCHAN
    position = np.arange(length, dtype=np.float64)
    centred = (position - (length - 1) / 2.0) / NCHAN
    window = 0.54 - 0.46 * np.cos(2.0 * np.pi * position / (length - 1))
    shaped = np.sinc(centred) * window
    shaped = shaped * np.sqrt(NCHAN / np.sum(shaped * shaped))
    rows = shaped.reshape(TAPS, LOW, 1, HIGH)
    return np.broadcast_to(rows, (TAPS, LOW, 2, HIGH)).reshape(TAPS, 2 * LOW, HIGH).astype(np.float32)


def split_table(table):
    high = table.astype(np.float32).astype(jnp.bfloat16)
    low = (table - high.astype(np.float64)).astype(np.float32).astype(jnp.bfloat16)
    return np.stack([high, low])


def first_table():
    angle = 2.0 * np.pi * (np.outer(np.arange(LOW), np.arange(LOW)) % LOW) / LOW
    turn = np.empty((2, LOW, LOW, 2))
    turn[0, :, :, 0] = np.cos(angle)
    turn[0, :, :, 1] = np.sin(angle)
    turn[1, :, :, 0] = -np.sin(angle)
    turn[1, :, :, 1] = np.cos(angle)
    full = np.zeros((2, LOW, BLOCK, BLOCK, LOW, 2))
    for frame in range(BLOCK):
        full[:, :, frame, frame] = turn
    side = 2 * LOW * BLOCK
    return split_table(full.reshape(side, side))


def twist_table():
    angle = 2.0 * np.pi * np.outer(np.arange(LOW), np.arange(HIGH)) / NCHAN
    both = np.stack([np.cos(angle), np.sin(angle)])
    return np.repeat(both, BLOCK, axis=1).astype(np.float32)


def second_table():
    angle = 2.0 * np.pi * (np.outer(np.arange(HIGH), np.arange(HIGH)) % HIGH) / HIGH
    top = np.concatenate([np.cos(angle), -np.sin(angle)], axis=1)
    bottom = np.concatenate([np.sin(angle), np.cos(angle)], axis=1)
    return split_table(np.concatenate([top, bottom], axis=0) / np.sqrt(NCHAN))


def dot(a, b):
    return jnp.dot(a, b, preferred_element_type=F32)


def kernel(
    tm_size, frames, trials,
    volt, delays, mask, coef, first, twist, second,
    zout, stats_out,
    x, c, b1, tw, b2, dl, mk, wh, wl, det, dt32, dtm, acc, part, parts_in, st_b, st_c, ser,
    load_sem, halo_send, halo_recv, part_send, part_recv, b_send, b_recv, c_send, c_recv,
):
    me = lax.axis_index("tm")
    hist = TAPS - 1
    rings = tm_size // GROUP
    row, col = me // GROUP, me % GROUP

    def peer(step):
        return lax.rem(me + step + tm_size, tm_size)

    def group_peer(step):
        return row * GROUP + lax.rem(col + step, GROUP)

    def ring_peer(step):
        return lax.rem(row + step, rings) * GROUP + col

    loads = [
        pltpu.make_async_copy(volt.at[p], x.at[p, pl.ds(hist, frames)], load_sem.at[p]) for p in range(2)
    ]
    for k, (source, target) in enumerate(
        [(coef, c), (first, b1), (twist, tw), (second, b2), (delays, dl), (mask, mk)]
    ):
        loads.append(pltpu.make_async_copy(source, target, load_sem.at[2 + k]))
    for load in loads:
        load.start()

    barrier = pltpu.get_barrier_semaphore()
    known = [peer(s) for k in range(1, DSPAN + 1) for s in (k, -k)]
    known += [group_peer(s) for s in range(1, GROUP)]
    known += [ring_peer(s) for s in range(1, rings)]
    for target in known:
        pl.semaphore_signal(barrier, inc=1, device_id={"tm": target}, device_id_type=MESH)
    loads[0].wait()
    loads[1].wait()
    pl.semaphore_wait(barrier, len(known))

    halos = []
    for p in range(2):
        halos.append(
            pltpu.make_async_remote_copy(
                src_ref=x.at[p, pl.ds(frames, hist)],
                dst_ref=x.at[p, pl.ds(0, hist)],
                send_sem=halo_send.at[p],
                recv_sem=halo_recv.at[p],
                device_id={"tm": peer(1)},
                device_id_type=MESH,
            )
        )
        halos[p].start()

    for load in loads[2:]:
        load.wait()

    def weigh(block):
        def step(k, carry):
            p, r = k // 2, k % 2
            rows = pl.ds(pl.multiple_of(r * 16, 16), 16)
            lanes = pl.ds(pl.multiple_of(p * LANES, LANES), LANES)
            sums = [None] * BLOCK
            for i in range(BLOCK + hist):
                value = x[p, block * BLOCK + i, rows, :].astype(F32)
                for f in range(BLOCK):
                    tap = i - f
                    if 0 <= tap < TAPS:
                        term = c[tap, rows, :] * value
                        sums[f] = term if tap == 0 else sums[f] + term
                        if tap == TAPS - 1:
                            high = sums[f].astype(BF16)
                            low = (sums[f] - high.astype(F32)).astype(BF16)
                            place = pl.ds(pl.multiple_of(f * 32 + r * 16, 16), 16)
                            wh[block, place, lanes] = high
                            wl[block, place, lanes] = low
            return carry

        lax.fori_loop(0, 4, step, 0)

    def transform(block):
        half = LOW * BLOCK
        z = dot(b1[0], wh[block]) + dot(b1[0], wl[block]) + dot(b1[1], wh[block])
        energy = None
        for p in range(2):
            zr = z[:half, p * LANES : (p + 1) * LANES]
            zi = z[half:, p * LANES : (p + 1) * LANES]
            turned = jnp.concatenate([zr * tw[0] + zi * tw[1], zi * tw[0] - zr * tw[1]], axis=1)
            high = turned.astype(BF16)
            low = (turned - high.astype(F32)).astype(BF16)
            u = dot(high, b2[0]) + dot(high, b2[1]) + dot(low, b2[0])
            power = u[:, :HIGH] * u[:, :HIGH] + u[:, HIGH:] * u[:, HIGH:]
            energy = power if p == 0 else energy + power
        for k in range(LOW):
            det[pl.ds(pl.multiple_of(block * BLOCK, BLOCK), BLOCK), k * HIGH : (k + 1) * HIGH] = energy[
                k * BLOCK : (k + 1) * BLOCK
            ]

    def blocks(begin, end):
        def step(block, carry):
            weigh(block)
            transform(block)
            return carry

        lax.fori_loop(begin, end, step, 0)

    blocks(2, 4)

    used = jnp.where(mk[...] > 0, dl[...], -1).astype(F32).astype(BF16)
    lane = lax.broadcasted_iota(jnp.int32, (trials, LANES), 1)
    trial = lax.broadcasted_iota(jnp.int32, (trials, LANES), 0)
    spread = (lax.rem(lane, trials) == trial).astype(F32).astype(BF16)
    dt32[...] = lax.dot_general(used, spread, (((0,), (0,)), ((), ())), preferred_element_type=F32)
    lane_k = lax.broadcasted_iota(jnp.int32, (HIGH, LANES), 1)
    offset = (lane_k // trials).astype(F32)
    for k in range(LOW):
        rows = dt32[pl.ds(k, HIGH, stride=LOW), :] - offset
        dtm[k * HIGH : (k + 1) * HIGH, :LANES] = rows.astype(BF16)
        dtm[k * HIGH : (k + 1) * HIGH, LANES:] = (rows - 2.0).astype(BF16)
    acc[...] = jnp.zeros_like(acc)

    for p in range(2):
        halos[p].wait_recv()

    @pl.when(me == 0)
    def _():
        x[:, :hist] = jnp.zeros((2, hist, 2 * LOW, HIGH), BF16)

    blocks(0, 2)

    span = DSPAN * frames
    chunk = 2 * HIGH

    def shift(a, carry):
        begin = pl.multiple_of(span - 8 * a, 8)
        for h in range(2):
            target = jnp.full((chunk, 2 * LANES), (8 * a + 4 * h).astype(F32)).astype(BF16)
            total = None
            for k in range(NCHAN // chunk):
                chosen = jnp.where(dtm[k * chunk : (k + 1) * chunk, :] == target, 1.0, 0.0).astype(BF16)
                term = dot(det[:, k * chunk : (k + 1) * chunk].astype(BF16), chosen)
                total = term if k == 0 else total + term
            acc[h, pl.ds(begin, frames), :] += total
        return carry

    lax.fori_loop(0, span // 8 + 1, shift, 0)

    even, odd = None, None
    rows_out = span + frames
    for h in range(2):
        for half in range(2):
            lanes = slice(half * LANES, (half + 1) * LANES)
            first_row = 4 * h + 2 * half
            left = acc[h, first_row : first_row + rows_out, lanes]
            right = acc[h, first_row + 1 : first_row + 1 + rows_out, lanes]
            even = left if even is None else even + left
            odd = right if odd is None else odd + right
    part[...] = even + pltpu.roll(odd, trials, 1)

    sends = []
    for k in range(1, DSPAN + 1):
        begin = span - k * frames
        copy = pltpu.make_async_remote_copy(
            src_ref=part.at[pl.ds(begin, frames)],
            dst_ref=parts_in.at[k - 1],
            send_sem=part_send.at[k - 1],
            recv_sem=part_recv.at[k - 1],
            device_id={"tm": peer(-k)},
            device_id_type=MESH,
        )
        copy.start()
        sends.append(copy)
    series = part[span:, :]
    for k in range(1, DSPAN + 1):
        sends[k - 1].wait_recv()
        inside = (me + k < tm_size).astype(F32)
        series = series + parts_in[k - 1] * inside

    def gather(slots, own, steps, to, send, recv):
        slots[0] = own
        copies = []
        for s in range(1, steps):
            copy = pltpu.make_async_remote_copy(
                src_ref=slots.at[0],
                dst_ref=slots.at[s],
                send_sem=send.at[s - 1],
                recv_sem=recv.at[s - 1],
                device_id={"tm": to(s)},
                device_id_type=MESH,
            )
            copy.start()
            copies.append(copy)
        for copy in copies:
            copy.wait_recv()
        return copies

    def pack(mean, second, peak):
        wide = lax.broadcasted_iota(jnp.int32, (1, LANES), 1)
        head = jnp.where(wide < trials, mean, pltpu.roll(second, trials, 1))
        return jnp.concatenate([head, peak], axis=0)

    def merge(slots, steps, count):
        heads = jnp.concatenate([slots[s, 0:1] for s in range(steps)], axis=0)
        peaks = jnp.concatenate([slots[s, 1:2] for s in range(steps)], axis=0)
        mean = jnp.sum(heads, axis=0, keepdims=True) / steps
        away = heads - mean
        seconds = pltpu.roll(mean * steps, trials, 1)
        second = seconds + count * jnp.sum(away * away, axis=0, keepdims=True)
        return mean, second, jnp.max(peaks, axis=0, keepdims=True)

    mean = jnp.sum(series, axis=0, keepdims=True) / frames
    away = series - mean
    second_sum = jnp.sum(away * away, axis=0, keepdims=True)
    peak = jnp.max(series, axis=0, keepdims=True)
    ser[...] = series
    b_copies = gather(st_b, pack(mean, second_sum, peak), GROUP, group_peer, b_send, b_recv)
    mean, second_sum, peak = merge(st_b, GROUP, float(frames))
    c_copies = gather(st_c, pack(mean, second_sum, peak), rings, ring_peer, c_send, c_recv)
    average, second_sum, peak = merge(st_c, rings, float(frames * GROUP))

    variance = second_sum / (frames * tm_size)
    deviation = jnp.sqrt(variance + 1e-05)
    z = (ser[...] - average) / deviation
    zout[...] = z[:, :trials]
    live = jnp.maximum(jnp.sum(mk[...].astype(F32)), 1.0)
    rows = jnp.concatenate([average / live, deviation / live, (peak - average) / deviation], axis=0)
    stats_out[...] = rows[:, :trials]

    for p in range(2):
        halos[p].wait_send()
    for copy in sends + b_copies + c_copies:
        copy.wait_send()


def per_device(tm_size, voltage, delays, chan_mask):
    frames = voltage.shape[2] // NCHAN
    trials = delays.shape[0]
    rows = voltage.shape[2] // HIGH
    volt = voltage.reshape(2, 2, rows, HIGH).transpose(0, 2, 1, 3).reshape(2, frames, 2 * LOW, HIGH)
    hist = TAPS - 1
    rings = tm_size // GROUP
    side = 2 * LOW * BLOCK
    vmem = pltpu.VMEM
    dma = pltpu.SemaphoreType.DMA
    span = DSPAN * frames
    zscore, stats = pl.pallas_call(
        functools.partial(kernel, tm_size, frames, trials),
        out_shape=(
            jax.ShapeDtypeStruct((frames, trials), F32),
            jax.ShapeDtypeStruct((3, trials), F32),
        ),
        in_specs=[pl.BlockSpec(memory_space=pl.ANY)] * 7,
        out_specs=(pl.BlockSpec(memory_space=pltpu.VMEM),) * 2,
        scratch_shapes=[
            vmem((2, hist + frames, 2 * LOW, HIGH), BF16),
            vmem((TAPS, 2 * LOW, HIGH), F32),
            vmem((2, side, side), BF16),
            vmem((2, LOW * BLOCK, HIGH), F32),
            vmem((2, 2 * HIGH, 2 * HIGH), BF16),
            vmem((trials, NCHAN), jnp.int32),
            vmem((1, NCHAN), jnp.int32),
            vmem((frames // BLOCK, side, 2 * LANES), BF16),
            vmem((frames // BLOCK, side, 2 * LANES), BF16),
            vmem((frames, NCHAN), F32),
            vmem((NCHAN, LANES), F32),
            vmem((NCHAN, 2 * LANES), BF16),
            vmem((2, span + frames + 8, 2 * LANES), F32),
            vmem((span + frames, LANES), F32),
            vmem((DSPAN, frames, LANES), F32),
            vmem((GROUP, 2, LANES), F32),
            vmem((rings, 2, LANES), F32),
            vmem((frames, LANES), F32),
            dma((8,)),
            dma((2,)),
            dma((2,)),
            dma((DSPAN,)),
            dma((DSPAN,)),
            dma((GROUP - 1,)),
            dma((GROUP - 1,)),
            dma((rings - 1,)),
            dma((rings - 1,)),
        ],
        compiler_params=pltpu.CompilerParams(
            collective_id=0, has_side_effects=True, vmem_limit_bytes=67043328
        ),
    )(
        volt, delays, chan_mask.reshape(1, NCHAN),
        jnp.asarray(filter_table()), jnp.asarray(first_table()),
        jnp.asarray(twist_table()), jnp.asarray(second_table()),
    )
    return zscore.T, stats


def solution(mesh):
    return jax.shard_map(
        functools.partial(per_device, mesh.shape["tm"]),
        mesh=mesh,
        in_specs=(P(None, None, ("beam", "tm")), P(), P("beam")),
        out_specs=(P(None, ("beam", "tm")), P(None, "beam")),
        check_vma=False,
    )
```

time: 124 us -> 53.7 us (0.43)
  Pallas kernels: 0 us -> 50.9 us
  blocking collectives: 43.1 us -> 0 us
  waiting for transfers between devices: 31.9 us -> 0 us
  matrix products: 17.3 us -> 0 us
  starting transfers between devices: 11.6 us -> 0 us
  other arithmetic: 8.32 us -> 0 us
  local copies, waits for them, and re-layouts: 7.22 us -> 1.91 us
  loops' own time: 1.66 us -> 0 us
  between operations: 2.27 us -> 0.65 us
    pallas_call x0 -> x1, Pallas kernels: none -> 50.9 us  [per_device(): pl.pallas_call(functools.partial(kernel, tm_size, frames, trials), out_sh...]
    all_gather x3 -> x0, blocking collectives: 43.1 us -> none  [all_in_one(): both, at, found = (lax.all_gather(jnp.concatenate(lines), axis), 0, {})]
    ppermute x3 -> x0, waiting for transfers between devices: 31.9 us -> none  [passed_along(): lax.ppermute(value, axis, [(source, source + steps) for source in range(f...]
    dot_general x21 -> x0, matrix products: 17.3 us -> none  [the longest x13 11.5 us: add_group(): jnp.einsum('dsk,skt->dt', selector, stacked, preferred_element_type=jnp.f...]
    ppermute x3 -> x0, starting transfers between devices: 11.6 us -> none  [passed_along(): lax.ppermute(value, axis, [(source, source + steps) for source in range(f...]
    while x91 -> x0, local copies, waits for them, and re-layouts: 3.45 us -> none
    add x19 -> x0, other arithmetic: 2.78 us -> none  [the longest x1 2.59 us: per_device(): weighted + coeffs[tap_index] * extended[:, :, tap_index:tap_index + frame...]
    reduce_sum x4 -> x0, other arithmetic: 1.92 us -> none  [the longest x1 1.24 us: prototype(): shaped = shaped * jnp.sqrt(chan_count / jnp.sum(shaped * shaped))]
  transfers between devices with their start and end apart: 3 -> 0, of which waited for: 3 -> 0; matrix products, arithmetic and copies ran while one was open for 2% -> 0% of each run, Pallas kernels for 0% -> 0%
where the time goes in v1:
time: 53.7 us; the launch traced here: 53.5 us
  Pallas kernels  50.9 us (95%)
  local copies, waits for them, and re-layouts  1.91 us (4%)
  between operations  0.65 us (1%)
    pallas_call x1, Pallas kernels, per_device(): pl.pallas_call(functools.partial(kernel, tm_size, frames, trials), out_sh...  50.9 us
    unnamed x4, local copies, waits for them, and re-layouts  1.91 us

profile of v1, /device:TPU:513, one launch (start us, length us, event | category | flops | bytes accessed | tf_op | source)
XLA Modules:
  0.0 53.5 jit_solution(11393576987218372013)
XLA Ops:
  0.6 50.9 %shard_map.86 = (f32[32,64]{1,0:T(8,128)}, f32[3,64]{1,0:T(4,128)}) custom-call(bf16[2,32,32,128]{3,2,1,0:T(8,128)(2,1)} %bitcast.7, s32[64,2048]{1,0:T(8,128)} %delays.1, s32[1,2048]{1,0:T(1,128)} %bitcast.9, f32[16,32,128]{2,1,0:T(8,128)} %constant.8.clone.coef, bf16[2,256,256]{2,1,0:T(8,128)(2,1)} %constant.9.clone.first, ...), custom_call_target="tpu_custom_call" | custom-call | tf_op jit(solution)/shard_map/pallas_call | solution.py:318
  51.6 0.0 copy-start
  51.6 1.3 %copy.12 = f32[64,32]{0,1:T(8,128)} copy(f32[64,32]{0,1:T(8,128)} %bitcast.8) | data formatting | bytes 16384
  52.9 0.0 copy-done
  52.9 0.6 %copy.13 = f32[3,64]{1,0:T(4,128)} copy(f32[3,64]{1,0:T(4,128)S(1)} %copy-done) | data formatting | bytes 1536
Async XLA Ops:
  51.6 1.3 %copy-start = (f32[3,64]{1,0:T(4,128)S(1)}, f32[3,64]{1,0:T(4,128)}, u32[]{:S(2)}) copy-start(f32[3,64]{1,0:T(4,128)} %get-tuple-element.9) | copy-start | bytes 2308

commit v2 on v1

v2 whole, which is shorter than its diff:
```python
import functools

import jax
import jax.numpy as jnp
import numpy as np
from jax import lax
from jax.experimental import pallas as pl
from jax.experimental.pallas import tpu as pltpu
from jax.sharding import PartitionSpec as P

NCHAN = 2048
TAPS = 16
LOW = 16
HIGH = 128
BLOCK = 8
GROUP = 16
LANES = 128
DSPAN = 3
CORES = 2
AHEAD = 4
MESH = pl.DeviceIdType.MESH
F32 = jnp.float32
BF16 = jnp.bfloat16


def filter_table():
    length = TAPS * NCHAN
    position = np.arange(length, dtype=np.float64)
    centred = (position - (length - 1) / 2.0) / NCHAN
    window = 0.54 - 0.46 * np.cos(2.0 * np.pi * position / (length - 1))
    shaped = np.sinc(centred) * window
    shaped = shaped * np.sqrt(NCHAN / np.sum(shaped * shaped))
    rows = shaped.reshape(TAPS, LOW, 1, HIGH)
    return np.broadcast_to(rows, (TAPS, LOW, 2, HIGH)).reshape(TAPS, 2 * LOW, HIGH).astype(np.float32)


def split_table(table):
    high = table.astype(np.float32).astype(jnp.bfloat16)
    low = (table - high.astype(np.float64)).astype(np.float32).astype(jnp.bfloat16)
    return np.stack([high, low])


def first_table():
    angle = 2.0 * np.pi * (np.outer(np.arange(LOW), np.arange(LOW)) % LOW) / LOW
    turn = np.empty((2, LOW, LOW, 2))
    turn[0, :, :, 0] = np.cos(angle)
    turn[0, :, :, 1] = np.sin(angle)
    turn[1, :, :, 0] = -np.sin(angle)
    turn[1, :, :, 1] = np.cos(angle)
    full = np.zeros((2, LOW, BLOCK, BLOCK, LOW, 2))
    for frame in range(BLOCK):
        full[:, :, frame, frame] = turn
    side = 2 * LOW * BLOCK
    return split_table(full.reshape(side, side))


def twist_table():
    angle = 2.0 * np.pi * np.outer(np.arange(LOW), np.arange(HIGH)) / NCHAN
    both = np.stack([np.cos(angle), np.sin(angle)])
    return np.repeat(both, BLOCK, axis=1).astype(np.float32)


def second_table():
    angle = 2.0 * np.pi * (np.outer(np.arange(HIGH), np.arange(HIGH)) % HIGH) / HIGH
    top = np.concatenate([np.cos(angle), -np.sin(angle)], axis=1)
    bottom = np.concatenate([np.sin(angle), np.cos(angle)], axis=1)
    return split_table(np.concatenate([top, bottom], axis=0) / np.sqrt(NCHAN))


def dot(a, b):
    return jnp.dot(a, b, preferred_element_type=F32)


def kernel(
    tm_size, frames, trials,
    volt, delays, mask, coef, first, twist, second,
    zout, stats_out,
    x, c, b1, tw, b2, dl, mk, wh, wl, det, dt32, dtm, acc, part, parts_in, st_a, st_b, st_c,
    load_sem, near_sem, past_sem, halo_send, halo_recv, part_send, part_recv, pair_send, pair_recv,
    b_send, b_recv, c_send, c_recv,
):
    me = lax.axis_index("tm")
    hist = TAPS - 1
    last = tm_size - 1
    rings = tm_size // GROUP
    side = GROUP // CORES
    core = lax.rem(me, CORES)
    place = me // CORES
    row, col = place // side, lax.rem(place, side)

    def signal(sem, target):
        pl.semaphore_signal(sem, inc=1, device_id={"tm": target}, device_id_type=MESH)

    def send(source, target, send_sem, recv_sem, device):
        return pltpu.make_async_remote_copy(
            src_ref=source, dst_ref=target, send_sem=send_sem, recv_sem=recv_sem,
            device_id={"tm": device}, device_id_type=MESH,
        )

    def col_peer(step):
        return (row * side + lax.rem(col + step, side)) * CORES + 1

    def row_peer(step, which):
        return (lax.rem(row + step, rings) * side + col) * CORES + which

    barrier = pltpu.get_barrier_semaphore()

    @pl.when(core == 1)
    def _():
        signal(barrier, me - 1)

        @pl.when(me < last)
        def _():
            signal(barrier, me + 1)

    loads = [
        pltpu.make_async_copy(volt.at[p], x.at[p, pl.ds(hist, frames)], load_sem.at[p]) for p in range(2)
    ]
    for k, (source, target) in enumerate(
        [(coef, c), (first, b1), (twist, tw), (second, b2), (delays, dl), (mask, mk)]
    ):
        loads.append(pltpu.make_async_copy(source, target, load_sem.at[2 + k]))
    for load in loads:
        load.start()

    @pl.when(core == 0)
    def _():
        pl.semaphore_wait(barrier, 1 + jnp.minimum(me, 1))
        signal(near_sem, me + 1)

        @pl.when(me > 0)
        def _():
            signal(near_sem, me - 1)

    def halo(k):
        p, rows = k // 2, pl.ds((k % 2) * 16, 16)
        return send(
            x.at[p, pl.ds(frames, hist), rows], x.at[p, pl.ds(0, hist), rows],
            halo_send.at[k], halo_recv.at[k], me + 1,
        )

    loads[0].wait()
    loads[1].wait()

    @pl.when(core == 1)
    def _():
        pl.semaphore_wait(near_sem, 1 + jnp.minimum(last - me, 1))

    @pl.when(me < last)
    def _():
        for k in range(4):
            halo(k).start()

    @pl.when(me == 0)
    def _():
        x[:, :hist] = jnp.zeros((2, hist, 2 * LOW, HIGH), BF16)

    @pl.when(core == 1)
    def _():
        for step in range(1, side):
            signal(barrier, col_peer(step))
        for step in range(1, rings):
            signal(barrier, row_peer(step, 1))

    for load in loads[2:]:
        load.wait()

    def weigh(block, k):
        p, r = k // 2, lax.rem(k, 2)
        rows = pl.ds(pl.multiple_of(r * 16, 16), 16)
        lanes = pl.ds(pl.multiple_of(p * LANES, LANES), LANES)
        sums = [None] * BLOCK
        for i in range(BLOCK + hist):
            value = x[p, block * BLOCK + i, rows, :].astype(F32)
            for f in range(BLOCK):
                tap = i - f
                if 0 <= tap < TAPS:
                    term = c[tap, rows, :] * value
                    sums[f] = term if tap == 0 else sums[f] + term
                    if tap == TAPS - 1:
                        high = sums[f].astype(BF16)
                        low = (sums[f] - high.astype(F32)).astype(BF16)
                        spot = pl.ds(pl.multiple_of(f * 32 + r * 16, 16), 16)
                        wh[block, spot, lanes] = high
                        wl[block, spot, lanes] = low

    def transform(pair):
        half = LOW * BLOCK
        energies = []
        turns = [
            dot(b1[0], wh[b]) + dot(b1[0], wl[b]) + dot(b1[1], wh[b]) for b in (2 * pair, 2 * pair + 1)
        ]
        for z in turns:
            energy = None
            for p in range(2):
                zr = z[:half, p * LANES : (p + 1) * LANES]
                zi = z[half:, p * LANES : (p + 1) * LANES]
                turned = jnp.concatenate([zr * tw[0] + zi * tw[1], zi * tw[0] - zr * tw[1]], axis=1)
                high = turned.astype(BF16)
                low = (turned - high.astype(F32)).astype(BF16)
                u = dot(high, b2[0]) + dot(high, b2[1]) + dot(low, b2[0])
                power = u[:, :HIGH] * u[:, :HIGH] + u[:, HIGH:] * u[:, HIGH:]
                energy = power if p == 0 else energy + power
            energies.append(energy)
        for k in range(LOW):
            both = jnp.concatenate([e[k * BLOCK : (k + 1) * BLOCK] for e in energies], axis=0)
            det[2 * pair * BLOCK : 2 * (pair + 1) * BLOCK, k * HIGH : (k + 1) * HIGH] = both.astype(BF16)

    def late_half(k, carry):
        weigh(2, k)
        weigh(3, k)
        return carry

    lax.fori_loop(0, 4, late_half, 0)
    transform(1)

    used = jnp.where(mk[...] > 0, dl[...], -1).astype(F32).astype(BF16)
    lane = lax.broadcasted_iota(jnp.int32, (trials, LANES), 1)
    trial = lax.broadcasted_iota(jnp.int32, (trials, LANES), 0)
    spread = (lax.rem(lane, trials) == trial).astype(F32).astype(BF16)
    dt32[...] = lax.dot_general(used, spread, (((0,), (0,)), ((), ())), preferred_element_type=F32)
    lane_k = lax.broadcasted_iota(jnp.int32, (HIGH, LANES), 1)
    offset = (lane_k // trials).astype(F32)
    for k in range(LOW):
        rows = dt32[pl.ds(k, HIGH, stride=LOW), :] - offset
        dtm[k * HIGH : (k + 1) * HIGH, :LANES] = rows.astype(BF16)
        dtm[k * HIGH : (k + 1) * HIGH, LANES:] = (rows - 2.0).astype(BF16)
    acc[...] = jnp.zeros_like(acc)

    for k in range(4):

        @pl.when(me > 0)
        def _():
            halo(k).wait_recv()

        def early_half(block, carry):
            weigh(block, k)
            return carry

        lax.fori_loop(0, 2, early_half, 0)

    @pl.when(core == 0)
    def _():
        signal(past_sem, me + 1)

    transform(0)

    span = DSPAN * frames
    chunk = 2 * HIGH

    def select(base, h):
        target = jnp.full((chunk, 2 * LANES), base + 4.0 * h).astype(BF16)
        total = None
        for k in range(NCHAN // chunk):
            chosen = jnp.where(dtm[k * chunk : (k + 1) * chunk, :] == target, 1.0, 0.0).astype(BF16)
            term = dot(det[:, k * chunk : (k + 1) * chunk], chosen)
            total = term if k == 0 else total + term
        return total

    def shift(i, carry):
        totals = []
        for j in range(AHEAD):
            a = i * AHEAD + j
            totals.append([select((8 * a).astype(F32), h) for h in range(2)])
        for j in range(AHEAD):
            begin = pl.multiple_of(span - 8 * (i * AHEAD + j), 8)
            for h in range(2):
                acc[h, pl.ds(begin, frames), :] += totals[j][h]
        return carry

    lax.fori_loop(0, span // 8 // AHEAD, shift, 0)
    acc[0, 0:frames, :] += select(float(span), 0)

    even, odd = None, None
    rows_out = span + frames
    for h in range(2):
        for half in range(2):
            lanes = slice(half * LANES, (half + 1) * LANES)
            first_row = 4 * h + 2 * half
            left = acc[h, first_row : first_row + rows_out, lanes]
            right = acc[h, first_row + 1 : first_row + 1 + rows_out, lanes]
            even = left if even is None else even + left
            odd = right if odd is None else odd + right
    part[...] = even + pltpu.roll(odd, trials, 1)

    @pl.when(core == 1)
    def _():
        pl.semaphore_wait(past_sem, 1)

    def part_copy(k):
        return send(
            part.at[pl.ds(span - k * frames, frames)], parts_in.at[k - 1],
            part_send.at[k - 1], part_recv.at[k - 1], me - k,
        )

    for k in range(1, DSPAN + 1):

        @pl.when(me >= k)
        def _():
            part_copy(k).start()

        @pl.when(me + k > last)
        def _():
            parts_in[k - 1] = jnp.zeros((frames, LANES), F32)

    for k in range(1, DSPAN + 1):

        @pl.when(me + k <= last)
        def _():
            part_copy(k).wait_recv()

    series = part[span:, :]
    for k in range(DSPAN):
        series = series + parts_in[k]

    def pack(mean, second, peak):
        wide = lax.broadcasted_iota(jnp.int32, (1, LANES), 1)
        head = jnp.where(wide < trials, mean, pltpu.roll(second, trials, 1))
        return jnp.concatenate([head, peak], axis=0)

    def merge(slots, steps, count):
        heads = jnp.concatenate([slots[s, 0:1] for s in range(steps)], axis=0)
        peaks = jnp.concatenate([slots[s, 1:2] for s in range(steps)], axis=0)
        mean = jnp.sum(heads, axis=0, keepdims=True) / steps
        away = heads - mean
        second = pltpu.roll(mean * steps, trials, 1) + count * jnp.sum(away * away, axis=0, keepdims=True)
        return mean, second, jnp.max(peaks, axis=0, keepdims=True)

    mean = jnp.sum(series, axis=0, keepdims=True) / frames
    away = series - mean
    second_sum = jnp.sum(away * away, axis=0, keepdims=True)
    st_a[0] = pack(mean, second_sum, jnp.max(series, axis=0, keepdims=True))

    pair = send(st_a.at[0], st_a.at[1], pair_send, pair_recv, me + 1)

    @pl.when(core == 0)
    def _():
        pair.start()

    @pl.when(core == 1)
    def _():
        pair.wait_recv()
        st_b[0] = pack(*merge(st_a, CORES, float(frames)))
        pl.semaphore_wait(barrier, side - 1 + rings - 1)
        copies = [
            send(st_b.at[0], st_b.at[s], b_send.at[s - 1], b_recv.at[s - 1], col_peer(s))
            for s in range(1, side)
        ]
        for copy in copies:
            copy.start()
        for copy in copies:
            copy.wait_recv()
        st_c[0] = pack(*merge(st_b, side, float(frames * CORES)))
        spread_out = [
            send(st_c.at[0], st_c.at[s], c_send.at[2 * s + w], c_recv.at[s], row_peer(s, w))
            for s in range(1, rings)
            for w in (1, 0)
        ]
        spread_out.append(send(st_c.at[0], st_c.at[0], c_send.at[0], c_recv.at[0], me - 1))
        for copy in spread_out:
            copy.start()
        for s in range(1, rings):
            spread_out[2 * (s - 1)].wait_recv()

    @pl.when(core == 0)
    def _():
        for s in range(rings):
            send(st_c.at[0], st_c.at[s], c_send.at[s], c_recv.at[s], me + 1).wait_recv()

    average, second_sum, peak = merge(st_c, rings, float(frames * GROUP))
    variance = second_sum / (frames * tm_size)
    deviation = jnp.sqrt(variance + 1e-05)
    series = part[span:, :]
    for k in range(DSPAN):
        series = series + parts_in[k]
    z = (series - average) / deviation
    zout[...] = z[:, :trials]
    live = jnp.maximum(jnp.sum(mk[...].astype(F32)), 1.0)
    rows = jnp.concatenate([average / live, deviation / live, (peak - average) / deviation], axis=0)
    stats_out[...] = rows[:, :trials]

    @pl.when(me < last)
    def _():
        for k in range(4):
            halo(k).wait_send()

    for k in range(1, DSPAN + 1):

        @pl.when(me >= k)
        def _():
            part_copy(k).wait_send()

    @pl.when(core == 0)
    def _():
        pair.wait_send()

    @pl.when(core == 1)
    def _():
        for s in range(1, side):
            send(st_b.at[0], st_b.at[s], b_send.at[s - 1], b_recv.at[s - 1], col_peer(s)).wait_send()
        for s in range(1, rings):
            for w in (1, 0):
                send(st_c.at[0], st_c.at[s], c_send.at[2 * s + w], c_recv.at[s], row_peer(s, w)).wait_send()
        send(st_c.at[0], st_c.at[0], c_send.at[0], c_recv.at[0], me - 1).wait_send()


def per_device(tm_size, voltage, delays, chan_mask):
    frames = voltage.shape[2] // NCHAN
    trials = delays.shape[0]
    rows = voltage.shape[2] // HIGH
    volt = voltage.reshape(2, 2, rows, HIGH).transpose(0, 2, 1, 3).reshape(2, frames, 2 * LOW, HIGH)
    hist = TAPS - 1
    rings = tm_size // GROUP
    side = 2 * LOW * BLOCK
    vmem = pltpu.VMEM
    dma = pltpu.SemaphoreType.DMA
    span = DSPAN * frames
    zscore, stats = pl.pallas_call(
        functools.partial(kernel, tm_size, frames, trials),
        out_shape=(
            jax.ShapeDtypeStruct((frames, trials), F32),
            jax.ShapeDtypeStruct((3, trials), F32),
        ),
        in_specs=[pl.BlockSpec(memory_space=pl.ANY)] * 7,
        out_specs=(pl.BlockSpec(memory_space=pltpu.VMEM),) * 2,
        scratch_shapes=[
            vmem((2, hist + frames, 2 * LOW, HIGH), BF16),
            vmem((TAPS, 2 * LOW, HIGH), F32),
            vmem((2, side, side), BF16),
            vmem((2, LOW * BLOCK, HIGH), F32),
            vmem((2, 2 * HIGH, 2 * HIGH), BF16),
            vmem((trials, NCHAN), jnp.int32),
            vmem((1, NCHAN), jnp.int32),
            vmem((frames // BLOCK, side, 2 * LANES), BF16),
            vmem((frames // BLOCK, side, 2 * LANES), BF16),
            vmem((frames, NCHAN), BF16),
            vmem((NCHAN, LANES), F32),
            vmem((NCHAN, 2 * LANES), BF16),
            vmem((2, span + frames + 8, 2 * LANES), F32),
            vmem((span + frames, LANES), F32),
            vmem((DSPAN, frames, LANES), F32),
            vmem((CORES, 2, LANES), F32),
            vmem((GROUP // CORES, 2, LANES), F32),
            vmem((rings, 2, LANES), F32),
            dma((8,)),
            pltpu.SemaphoreType.REGULAR,
            pltpu.SemaphoreType.REGULAR,
            dma((4,)),
            dma((4,)),
            dma((DSPAN,)),
            dma((DSPAN,)),
            dma,
            dma,
            dma((GROUP // CORES - 1,)),
            dma((GROUP // CORES - 1,)),
            dma((2 * rings,)),
            dma((rings,)),
        ],
        compiler_params=pltpu.CompilerParams(
            collective_id=0, has_side_effects=True, vmem_limit_bytes=67043328
        ),
    )(
        volt, delays, chan_mask.reshape(1, NCHAN),
        jnp.asarray(filter_table()), jnp.asarray(first_table()),
        jnp.asarray(twist_table()), jnp.asarray(second_table()),
    )
    return zscore.T, stats


def solution(mesh):
    return jax.shard_map(
        functools.partial(per_device, mesh.shape["tm"]),
        mesh=mesh,
        in_specs=(P(None, None, ("beam", "tm")), P(), P("beam")),
        out_specs=(P(None, ("beam", "tm")), P(None, "beam")),
        check_vma=False,
    )
```

time: 53.7 us -> 47.2 us (0.88)
  Pallas kernels: 50.9 us -> 44.5 us
    pallas_call x1, Pallas kernels: 50.9 us -> 44.5 us  [per_device(): pl.pallas_call(functools.partial(kernel, tm_size, frames, trials), out_sh...]
where the time goes in v2:
time: 47.2 us; the launch traced here: 47.1 us
  Pallas kernels  44.5 us (94%)
  local copies, waits for them, and re-layouts  1.91 us (4%)
  between operations  0.65 us (1%)
    pallas_call x1, Pallas kernels, per_device(): pl.pallas_call(functools.partial(kernel, tm_size, frames, trials), out_sh...  44.5 us
    unnamed x4, local copies, waits for them, and re-layouts  1.91 us

profile of v2, /device:TPU:513, one launch (start us, length us, event | category | flops | bytes accessed | tf_op | source)
XLA Modules:
  0.0 47.1 jit_solution(437285424748631762)
XLA Ops:
  0.6 44.5 %shard_map.86 = (f32[32,64]{1,0:T(8,128)}, f32[3,64]{1,0:T(4,128)}) custom-call(bf16[2,32,32,128]{3,2,1,0:T(8,128)(2,1)} %bitcast.7, s32[64,2048]{1,0:T(8,128)} %delays.1, s32[1,2048]{1,0:T(1,128)} %bitcast.9, f32[16,32,128]{2,1,0:T(8,128)} %constant.8.clone.coef, bf16[2,256,256]{2,1,0:T(8,128)(2,1)} %constant.9.clone.first, ...), custom_call_target="tpu_custom_call" | custom-call | tf_op jit(solution)/shard_map/pallas_call | solution.py:418
  45.1 0.0 copy-start
  45.2 1.3 %copy.12 = f32[64,32]{0,1:T(8,128)} copy(f32[64,32]{0,1:T(8,128)} %bitcast.8) | data formatting | bytes 16384
  46.5 0.0 copy-done
  46.5 0.6 %copy.13 = f32[3,64]{1,0:T(4,128)} copy(f32[3,64]{1,0:T(4,128)S(1)} %copy-done) | data formatting | bytes 1536
Async XLA Ops:
  45.1 1.3 %copy-start = (f32[3,64]{1,0:T(4,128)S(1)}, f32[3,64]{1,0:T(4,128)}, u32[]{:S(2)}) copy-start(f32[3,64]{1,0:T(4,128)} %get-tuple-element.9) | copy-start | bytes 2308

commit v3 on v2

--- a/solution.py
+++ b/solution.py
@@ -21,6 +21,7 @@
 MESH = pl.DeviceIdType.MESH
 F32 = jnp.float32
 BF16 = jnp.bfloat16
+I16 = jnp.int16
 
 
 def filter_table():
@@ -75,9 +76,9 @@
     tm_size, frames, trials,
     volt, delays, mask, coef, first, twist, second,
     zout, stats_out,
-    x, c, b1, tw, b2, dl, mk, wh, wl, det, dt32, dtm, acc, part, parts_in, st_a, st_b, st_c,
+    x, c, b1, tw, b2, dl, mk, wh, wl, det, dt32, dtm, acc, part, parts_in, st_a, st_b,
     load_sem, near_sem, past_sem, halo_send, halo_recv, part_send, part_recv, pair_send, pair_recv,
-    b_send, b_recv, c_send, c_recv,
+    b_send, b_recv,
 ):
     me = lax.axis_index("tm")
     hist = TAPS - 1
@@ -86,7 +87,7 @@
     side = GROUP // CORES
     core = lax.rem(me, CORES)
     place = me // CORES
-    row, col = place // side, lax.rem(place, side)
+    chips = rings * side
 
     def signal(sem, target):
         pl.semaphore_signal(sem, inc=1, device_id={"tm": target}, device_id_type=MESH)
@@ -97,11 +98,17 @@
             device_id={"tm": device}, device_id_type=MESH,
         )
 
-    def col_peer(step):
-        return (row * side + lax.rem(col + step, side)) * CORES + 1
-
-    def row_peer(step, which):
-        return (lax.rem(row + step, rings) * side + col) * CORES + which
+    def every_chip(act):
+        def step(k, carry):
+            chip = lax.rem(k, rings) * side + k // rings
+
+            @pl.when(chip != place)
+            def _():
+                act(chip)
+
+            return carry
+
+        lax.fori_loop(0, chips, step, 0)
 
     barrier = pltpu.get_barrier_semaphore()
 
@@ -157,10 +164,7 @@
 
     @pl.when(core == 1)
     def _():
-        for step in range(1, side):
-            signal(barrier, col_peer(step))
-        for step in range(1, rings):
-            signal(barrier, row_peer(step, 1))
+        every_chip(lambda chip: signal(barrier, chip * CORES + 1))
 
     for load in loads[2:]:
         load.wait()
@@ -218,13 +222,14 @@
     lane = lax.broadcasted_iota(jnp.int32, (trials, LANES), 1)
     trial = lax.broadcasted_iota(jnp.int32, (trials, LANES), 0)
     spread = (lax.rem(lane, trials) == trial).astype(F32).astype(BF16)
+    live = jnp.maximum(jnp.sum(mk[...].astype(F32)), 1.0)
     dt32[...] = lax.dot_general(used, spread, (((0,), (0,)), ((), ())), preferred_element_type=F32)
     lane_k = lax.broadcasted_iota(jnp.int32, (HIGH, LANES), 1)
     offset = (lane_k // trials).astype(F32)
     for k in range(LOW):
         rows = dt32[pl.ds(k, HIGH, stride=LOW), :] - offset
-        dtm[k * HIGH : (k + 1) * HIGH, :LANES] = rows.astype(BF16)
-        dtm[k * HIGH : (k + 1) * HIGH, LANES:] = (rows - 2.0).astype(BF16)
+        dtm[k * HIGH : (k + 1) * HIGH, :LANES] = rows.astype(jnp.int32).astype(I16)
+        dtm[k * HIGH : (k + 1) * HIGH, LANES:] = (rows - 2.0).astype(jnp.int32).astype(I16)
     acc[...] = jnp.zeros_like(acc)
 
     for k in range(4):
@@ -248,11 +253,14 @@
     span = DSPAN * frames
     chunk = 2 * HIGH
 
+    ones = jnp.ones((chunk, 2 * LANES), BF16)
+    zeros = jnp.zeros((chunk, 2 * LANES), BF16)
+
     def select(base, h):
-        target = jnp.full((chunk, 2 * LANES), base + 4.0 * h).astype(BF16)
+        target = jnp.full((chunk, 2 * LANES), base + 4 * h, jnp.int32).astype(I16)
         total = None
         for k in range(NCHAN // chunk):
-            chosen = jnp.where(dtm[k * chunk : (k + 1) * chunk, :] == target, 1.0, 0.0).astype(BF16)
+            chosen = jnp.where(dtm[k * chunk : (k + 1) * chunk, :] == target, ones, zeros)
             term = dot(det[:, k * chunk : (k + 1) * chunk], chosen)
             total = term if k == 0 else total + term
         return total
@@ -261,7 +269,7 @@
         totals = []
         for j in range(AHEAD):
             a = i * AHEAD + j
-            totals.append([select((8 * a).astype(F32), h) for h in range(2)])
+            totals.append([select(8 * a, h) for h in range(2)])
         for j in range(AHEAD):
             begin = pl.multiple_of(span - 8 * (i * AHEAD + j), 8)
             for h in range(2):
@@ -269,7 +277,7 @@
         return carry
 
     lax.fori_loop(0, span // 8 // AHEAD, shift, 0)
-    acc[0, 0:frames, :] += select(float(span), 0)
+    acc[0, 0:frames, :] += select(span, 0)
 
     even, odd = None, None
     rows_out = span + frames
@@ -319,66 +327,45 @@
         return jnp.concatenate([head, peak], axis=0)
 
     def merge(slots, steps, count):
-        heads = jnp.concatenate([slots[s, 0:1] for s in range(steps)], axis=0)
-        peaks = jnp.concatenate([slots[s, 1:2] for s in range(steps)], axis=0)
-        mean = jnp.sum(heads, axis=0, keepdims=True) / steps
-        away = heads - mean
-        second = pltpu.roll(mean * steps, trials, 1) + count * jnp.sum(away * away, axis=0, keepdims=True)
-        return mean, second, jnp.max(peaks, axis=0, keepdims=True)
+        entries = slots[...]
+        mean = jnp.sum(entries, axis=0) / steps
+        away = entries - mean[None]
+        spread_sum = jnp.sum(away * away, axis=0)
+        second = pltpu.roll(mean * steps, trials, 1) + count * spread_sum
+        return mean[0:1], second[0:1], jnp.max(entries, axis=0)[1:2]
 
     mean = jnp.sum(series, axis=0, keepdims=True) / frames
     away = series - mean
     second_sum = jnp.sum(away * away, axis=0, keepdims=True)
     st_a[0] = pack(mean, second_sum, jnp.max(series, axis=0, keepdims=True))
-
-    pair = send(st_a.at[0], st_a.at[1], pair_send, pair_recv, me + 1)
-
-    @pl.when(core == 0)
-    def _():
-        pair.start()
+    part[span:, :] = series
 
     @pl.when(core == 1)
     def _():
-        pair.wait_recv()
-        st_b[0] = pack(*merge(st_a, CORES, float(frames)))
-        pl.semaphore_wait(barrier, side - 1 + rings - 1)
-        copies = [
-            send(st_b.at[0], st_b.at[s], b_send.at[s - 1], b_recv.at[s - 1], col_peer(s))
-            for s in range(1, side)
-        ]
-        for copy in copies:
-            copy.start()
-        for copy in copies:
-            copy.wait_recv()
-        st_c[0] = pack(*merge(st_b, side, float(frames * CORES)))
-        spread_out = [
-            send(st_c.at[0], st_c.at[s], c_send.at[2 * s + w], c_recv.at[s], row_peer(s, w))
-            for s in range(1, rings)
-            for w in (1, 0)
-        ]
-        spread_out.append(send(st_c.at[0], st_c.at[0], c_send.at[0], c_recv.at[0], me - 1))
-        for copy in spread_out:
-            copy.start()
-        for s in range(1, rings):
-            spread_out[2 * (s - 1)].wait_recv()
-
-    @pl.when(core == 0)
-    def _():
-        for s in range(rings):
-            send(st_c.at[0], st_c.at[s], c_send.at[s], c_recv.at[s], me + 1).wait_recv()
-
-    average, second_sum, peak = merge(st_c, rings, float(frames * GROUP))
+        pl.semaphore_wait(barrier, chips - 1)
+
+    pair = send(st_a.at[0], st_a.at[1], pair_send, pair_recv, me + 1 - 2 * core)
+    pair.start()
+    pair.wait_recv()
+    st_b[place] = pack(*merge(st_a, CORES, float(frames)))
+
+    def chip_copy(chip):
+        return send(st_b.at[place], st_b.at[place], b_send, b_recv, chip * CORES + core)
+
+    every_chip(lambda chip: chip_copy(chip).start())
+    others = st_b.at[pl.ds(0, chips - 1)]
+    pltpu.make_async_copy(others, others, b_recv).wait()
+
+    average, second_sum, peak = merge(st_b, chips, float(frames * CORES))
     variance = second_sum / (frames * tm_size)
     deviation = jnp.sqrt(variance + 1e-05)
-    series = part[span:, :]
-    for k in range(DSPAN):
-        series = series + parts_in[k]
-    z = (series - average) / deviation
-    zout[...] = z[:, :trials]
-    live = jnp.maximum(jnp.sum(mk[...].astype(F32)), 1.0)
+    zout[...] = ((part[span:, :] - average) / deviation)[:, :trials]
     rows = jnp.concatenate([average / live, deviation / live, (peak - average) / deviation], axis=0)
     stats_out[...] = rows[:, :trials]
 
+    pair.wait_send()
+    pltpu.make_async_copy(others, others, b_send).wait()
+
     @pl.when(me < last)
     def _():
         for k in range(4):
@@ -389,19 +376,6 @@
         @pl.when(me >= k)
         def _():
             part_copy(k).wait_send()
-
-    @pl.when(core == 0)
-    def _():
-        pair.wait_send()
-
-    @pl.when(core == 1)
-    def _():
-        for s in range(1, side):
-            send(st_b.at[0], st_b.at[s], b_send.at[s - 1], b_recv.at[s - 1], col_peer(s)).wait_send()
-        for s in range(1, rings):
-            for w in (1, 0):
-                send(st_c.at[0], st_c.at[s], c_send.at[2 * s + w], c_recv.at[s], row_peer(s, w)).wait_send()
-        send(st_c.at[0], st_c.at[0], c_send.at[0], c_recv.at[0], me - 1).wait_send()
 
 
 def per_device(tm_size, voltage, delays, chan_mask):
@@ -410,7 +384,6 @@
     rows = voltage.shape[2] // HIGH
     volt = voltage.reshape(2, 2, rows, HIGH).transpose(0, 2, 1, 3).reshape(2, frames, 2 * LOW, HIGH)
     hist = TAPS - 1
-    rings = tm_size // GROUP
     side = 2 * LOW * BLOCK
     vmem = pltpu.VMEM
     dma = pltpu.SemaphoreType.DMA
@@ -435,13 +408,12 @@
             vmem((frames // BLOCK, side, 2 * LANES), BF16),
             vmem((frames, NCHAN), BF16),
             vmem((NCHAN, LANES), F32),
-            vmem((NCHAN, 2 * LANES), BF16),
+            vmem((NCHAN, 2 * LANES), I16),
             vmem((2, span + frames + 8, 2 * LANES), F32),
             vmem((span + frames, LANES), F32),
             vmem((DSPAN, frames, LANES), F32),
             vmem((CORES, 2, LANES), F32),
-            vmem((GROUP // CORES, 2, LANES), F32),
-            vmem((rings, 2, LANES), F32),
+            vmem((tm_size // CORES, 2, LANES), F32),
             dma((8,)),
             pltpu.SemaphoreType.REGULAR,
             pltpu.SemaphoreType.REGULAR,
@@ -451,10 +423,8 @@
             dma((DSPAN,)),
             dma,
             dma,
-            dma((GROUP // CORES - 1,)),
-            dma((GROUP // CORES - 1,)),
-            dma((2 * rings,)),
-            dma((rings,)),
+            dma,
+            dma,
         ],
         compiler_params=pltpu.CompilerParams(
             collective_id=0, has_side_effects=True, vmem_limit_bytes=67043328

time: 47.2 us -> 44.3 us (0.939)
  Pallas kernels: 44.5 us -> 41.3 us
    pallas_call x1, Pallas kernels: 44.5 us -> 41.3 us  [per_device(): pl.pallas_call(functools.partial(kernel, tm_size, frames, trials), out_sh...]
where the time goes in v3:
time: 44.3 us; the launch traced here: 43.8 us
  Pallas kernels  41.3 us (93%)
  local copies, waits for them, and re-layouts  1.91 us (4%)
  between operations  0.65 us (1%)
    pallas_call x1, Pallas kernels, per_device(): pl.pallas_call(functools.partial(kernel, tm_size, frames, trials), out_sh...  41.3 us
    unnamed x4, local copies, waits for them, and re-layouts  1.91 us

profile of v3, /device:TPU:513, one launch (start us, length us, event | category | flops | bytes accessed | tf_op | source)
XLA Modules:
  0.0 43.8 jit_solution(5366117907723965671)
XLA Ops:
  0.6 41.3 %shard_map.86 = (f32[32,64]{1,0:T(8,128)}, f32[3,64]{1,0:T(4,128)}) custom-call(bf16[2,32,32,128]{3,2,1,0:T(8,128)(2,1)} %bitcast.7, s32[64,2048]{1,0:T(8,128)} %delays.1, s32[1,2048]{1,0:T(1,128)} %bitcast.9, f32[16,32,128]{2,1,0:T(8,128)} %constant.8.clone.coef, bf16[2,256,256]{2,1,0:T(8,128)(2,1)} %constant.9.clone.first, ...), custom_call_target="tpu_custom_call" | custom-call | tf_op jit(solution)/shard_map/pallas_call | solution.py:391
  41.9 0.0 copy-start
  41.9 1.3 %copy.12 = f32[64,32]{0,1:T(8,128)} copy(f32[64,32]{0,1:T(8,128)} %bitcast.8) | data formatting | bytes 16384
  43.2 0.0 copy-done
  43.3 0.6 %copy.13 = f32[3,64]{1,0:T(4,128)} copy(f32[3,64]{1,0:T(4,128)S(1)} %copy-done) | data formatting | bytes 1536
Async XLA Ops:
  41.9 1.3 %copy-start = (f32[3,64]{1,0:T(4,128)S(1)}, f32[3,64]{1,0:T(4,128)}, u32[]{:S(2)}) copy-start(f32[3,64]{1,0:T(4,128)} %get-tuple-element.9) | copy-start | bytes 2308

commit v4 on v3

--- a/solution.py
+++ b/solution.py
@@ -17,7 +17,7 @@
 LANES = 128
 DSPAN = 3
 CORES = 2
-AHEAD = 4
+SOME = 9
 MESH = pl.DeviceIdType.MESH
 F32 = jnp.float32
 BF16 = jnp.bfloat16
@@ -77,7 +77,7 @@
     volt, delays, mask, coef, first, twist, second,
     zout, stats_out,
     x, c, b1, tw, b2, dl, mk, wh, wl, det, dt32, dtm, acc, part, parts_in, st_a, st_b,
-    load_sem, near_sem, past_sem, halo_send, halo_recv, part_send, part_recv, pair_send, pair_recv,
+    load_sem, go_sem, all_sem, past_sem, past2_sem, halo_send, halo_recv, part_send, part_recv, pair_send, pair_recv,
     b_send, b_recv,
 ):
     me = lax.axis_index("tm")
@@ -100,44 +100,38 @@
 
     def every_chip(act):
         def step(k, carry):
-            chip = lax.rem(k, rings) * side + k // rings
-
-            @pl.when(chip != place)
-            def _():
-                act(chip)
-
+            for j in range(1, SOME + 1):
+                act(lax.rem(place + k * SOME + j, chips))
             return carry
 
-        lax.fori_loop(0, chips, step, 0)
+        lax.fori_loop(0, (chips - 1) // SOME, step, 0)
+        for j in range((chips - 1) // SOME * SOME + 1, chips):
+            act(lax.rem(place + j, chips))
 
     barrier = pltpu.get_barrier_semaphore()
 
-    @pl.when(core == 1)
+    @pl.when(me > 0)
     def _():
         signal(barrier, me - 1)
 
-        @pl.when(me < last)
-        def _():
-            signal(barrier, me + 1)
-
+    @pl.when(me > 1)
+    def _():
+        signal(barrier, 0)
+
+    early = frames - hist
     loads = [
-        pltpu.make_async_copy(volt.at[p], x.at[p, pl.ds(hist, frames)], load_sem.at[p]) for p in range(2)
+        pltpu.make_async_copy(
+            volt.at[p, pl.ds(begin, size)], x.at[p, pl.ds(hist + begin, size)], load_sem.at[2 * k + p]
+        )
+        for k, (begin, size) in enumerate([(early, hist), (0, early)])
+        for p in range(2)
     ]
     for k, (source, target) in enumerate(
         [(coef, c), (first, b1), (twist, tw), (second, b2), (delays, dl), (mask, mk)]
     ):
-        loads.append(pltpu.make_async_copy(source, target, load_sem.at[2 + k]))
+        loads.append(pltpu.make_async_copy(source, target, load_sem.at[4 + k]))
     for load in loads:
         load.start()
-
-    @pl.when(core == 0)
-    def _():
-        pl.semaphore_wait(barrier, 1 + jnp.minimum(me, 1))
-        signal(near_sem, me + 1)
-
-        @pl.when(me > 0)
-        def _():
-            signal(near_sem, me - 1)
 
     def halo(k):
         p, rows = k // 2, pl.ds((k % 2) * 16, 16)
@@ -149,9 +143,14 @@
     loads[0].wait()
     loads[1].wait()
 
-    @pl.when(core == 1)
-    def _():
-        pl.semaphore_wait(near_sem, 1 + jnp.minimum(last - me, 1))
+    @pl.when(me == 0)
+    def _():
+        pl.semaphore_wait(barrier, last)
+        signal(go_sem, 1)
+
+    @pl.when((me > 0) & (me < last))
+    def _():
+        pl.semaphore_wait(barrier, 1)
 
     @pl.when(me < last)
     def _():
@@ -161,10 +160,6 @@
     @pl.when(me == 0)
     def _():
         x[:, :hist] = jnp.zeros((2, hist, 2 * LOW, HIGH), BF16)
-
-    @pl.when(core == 1)
-    def _():
-        every_chip(lambda chip: signal(barrier, chip * CORES + 1))
 
     for load in loads[2:]:
         load.wait()
@@ -232,6 +227,12 @@
         dtm[k * HIGH : (k + 1) * HIGH, LANES:] = (rows - 2.0).astype(jnp.int32).astype(I16)
     acc[...] = jnp.zeros_like(acc)
 
+    @pl.when(me == 1)
+    def _():
+        pl.semaphore_wait(go_sem, 1)
+        signal(past_sem, 2)
+        signal(go_sem, DSPAN)
+
     for k in range(4):
 
         @pl.when(me > 0)
@@ -244,14 +245,26 @@
 
         lax.fori_loop(0, 2, early_half, 0)
 
-    @pl.when(core == 0)
+    @pl.when((me > 1) & (me < last))
     def _():
         signal(past_sem, me + 1)
 
     transform(0)
+
+    def hear(parity):
+        @pl.when((me > 1) & (core == parity))
+        def _():
+            pl.semaphore_wait(past_sem, 1)
+
+            @pl.when(me < last)
+            def _():
+                signal(past2_sem, me + 1)
+
+    hear(0)
 
     span = DSPAN * frames
     chunk = 2 * HIGH
+    ahead = frames // 8
 
     ones = jnp.ones((chunk, 2 * LANES), BF16)
     zeros = jnp.zeros((chunk, 2 * LANES), BF16)
@@ -267,17 +280,23 @@
 
     def shift(i, carry):
         totals = []
-        for j in range(AHEAD):
-            a = i * AHEAD + j
+        for j in range(ahead):
+            a = i * ahead + j
             totals.append([select(8 * a, h) for h in range(2)])
-        for j in range(AHEAD):
-            begin = pl.multiple_of(span - 8 * (i * AHEAD + j), 8)
+        for j in range(ahead):
+            begin = pl.multiple_of(span - 8 * (i * ahead + j), 8)
             for h in range(2):
                 acc[h, pl.ds(begin, frames), :] += totals[j][h]
         return carry
 
-    lax.fori_loop(0, span // 8 // AHEAD, shift, 0)
-    acc[0, 0:frames, :] += select(span, 0)
+    lax.fori_loop(0, jnp.minimum(me + 1, DSPAN), shift, 0)
+
+    @pl.when(me >= DSPAN)
+    def _():
+        acc[0, 0:frames, :] += select(span, 0)
+
+
+    hear(1)
 
     even, odd = None, None
     rows_out = span + frames
@@ -291,10 +310,6 @@
             odd = right if odd is None else odd + right
     part[...] = even + pltpu.roll(odd, trials, 1)
 
-    @pl.when(core == 1)
-    def _():
-        pl.semaphore_wait(past_sem, 1)
-
     def part_copy(k):
         return send(
             part.at[pl.ds(span - k * frames, frames)], parts_in.at[k - 1],
@@ -305,11 +320,28 @@
 
         @pl.when(me >= k)
         def _():
+            if k == DSPAN:
+                pl.semaphore_wait(past2_sem, 1)
             part_copy(k).start()
 
         @pl.when(me + k > last)
         def _():
             parts_in[k - 1] = jnp.zeros((frames, LANES), F32)
+
+    @pl.when(me == DSPAN)
+    def _():
+        pl.semaphore_wait(go_sem, 1)
+
+        def tell(k, carry):
+            for j in range(SOME):
+                signal(all_sem, DSPAN + 1 + k * SOME + j)
+            return carry
+
+        others = tm_size - 1 - DSPAN
+        signal(all_sem, 2)
+        lax.fori_loop(0, others // SOME, tell, 0)
+        for j in range(others // SOME * SOME, others):
+            signal(all_sem, DSPAN + 1 + j)
 
     for k in range(1, DSPAN + 1):
 
@@ -340,9 +372,9 @@
     st_a[0] = pack(mean, second_sum, jnp.max(series, axis=0, keepdims=True))
     part[span:, :] = series
 
-    @pl.when(core == 1)
-    def _():
-        pl.semaphore_wait(barrier, chips - 1)
+    @pl.when((me > 1) & (me != DSPAN))
+    def _():
+        pl.semaphore_wait(all_sem, 1)
 
     pair = send(st_a.at[0], st_a.at[1], pair_send, pair_recv, me + 1 - 2 * core)
     pair.start()
@@ -414,7 +446,9 @@
             vmem((DSPAN, frames, LANES), F32),
             vmem((CORES, 2, LANES), F32),
             vmem((tm_size // CORES, 2, LANES), F32),
-            dma((8,)),
+            dma((10,)),
+            pltpu.SemaphoreType.REGULAR,
+            pltpu.SemaphoreType.REGULAR,
             pltpu.SemaphoreType.REGULAR,
             pltpu.SemaphoreType.REGULAR,
             dma((4,)),
@@ -427,12 +461,17 @@
             dma,
         ],
         compiler_params=pltpu.CompilerParams(
-            collective_id=0, has_side_effects=True, vmem_limit_bytes=67043328
+            collective_id=0, has_side_effects=True, vmem_limit_bytes=40 << 20
         ),
     )(
-        volt, delays, chan_mask.reshape(1, NCHAN),
-        jnp.asarray(filter_table()), jnp.asarray(first_table()),
-        jnp.asarray(twist_table()), jnp.asarray(second_table()),
+        *(
+            pltpu.with_memory_space_constraint(value, pltpu.HBM)
+            for value in (
+                volt, delays, chan_mask.reshape(1, NCHAN),
+                jnp.asarray(filter_table()), jnp.asarray(first_table()),
+                jnp.asarray(twist_table()), jnp.asarray(second_table()),
+            )
+        )
     )
     return zscore.T, stats
 

time: 44.3 us -> 40.8 us (0.921)
  Pallas kernels: 41.3 us -> 38.8 us
  local copies, waits for them, and re-layouts: 1.91 us -> 1.19 us
    pallas_call x1, Pallas kernels: 41.3 us -> 38.8 us  [per_device(): pl.pallas_call(functools.partial(kernel, tm_size, frames, trials), out_sh...]
    unnamed x4 -> x2, local copies, waits for them, and re-layouts: 1.91 us -> 1.19 us
where the time goes in v4:
time: 40.8 us; the launch traced here: 40.7 us
  Pallas kernels  38.8 us (95%)
  local copies, waits for them, and re-layouts  1.19 us (3%)
  between operations  0.64 us (2%)
    pallas_call x1, Pallas kernels, per_device(): pl.pallas_call(functools.partial(kernel, tm_size, frames, trials), out_sh...  38.8 us
    unnamed x2, local copies, waits for them, and re-layouts  1.19 us

profile of v4, /device:TPU:513, one launch (start us, length us, event | category | flops | bytes accessed | tf_op | source)
XLA Modules:
  0.0 40.7 jit_solution(2077281536178747683)
XLA Ops:
  0.6 38.8 %shard_map.86 = (f32[32,64]{1,0:T(8,128)S(1)}, f32[3,64]{1,0:T(4,128)S(1)}) custom-call(bf16[2,32,32,128]{3,2,1,0:T(8,128)(2,1)} %bitcast.8, s32[64,2048]{1,0:T(8,128)} %delays.1, s32[1,2048]{1,0:T(1,128)} %bitcast.9, f32[16,32,128]{2,1,0:T(8,128)} %constant.8.clone.coef, bf16[2,256,256]{2,1,0:T(8,128)(2,1)} %constant.9.clone.first, ...), custom_call_target="tpu_custom_call" | custom-call | tf_op jit(solution)/shard_map/pallas_call | solution.py:423
  39.5 0.6 %copy.12 = f32[64,32]{0,1:T(8,128)} copy(f32[64,32]{0,1:T(8,128)S(1)} %bitcast.7) | data formatting | bytes 16384
  40.1 0.6 %copy.13 = f32[3,64]{1,0:T(4,128)} copy(f32[3,64]{1,0:T(4,128)S(1)} %get-tuple-element.9) | data formatting | bytes 1536

commit v5 on v4

--- a/solution.py
+++ b/solution.py
@@ -22,6 +22,7 @@
 F32 = jnp.float32
 BF16 = jnp.bfloat16
 I16 = jnp.int16
+F8 = jnp.float8_e4m3fn
 
 
 def filter_table():
@@ -69,7 +70,15 @@
 
 
 def dot(a, b):
-    return jnp.dot(a, b, preferred_element_type=F32)
+    return lax.dot_general(a, b, (((1,), (0,)), ((), ())), preferred_element_type=F32)
+
+
+def hand_on(zscore, stats, zout, stats_out, sems):
+    copies = [pltpu.make_async_copy(zscore, zout, sems.at[0]), pltpu.make_async_copy(stats, stats_out, sems.at[1])]
+    for copy in copies:
+        copy.start()
+    for copy in copies:
+        copy.wait()
 
 
 def kernel(
@@ -227,6 +236,47 @@
         dtm[k * HIGH : (k + 1) * HIGH, LANES:] = (rows - 2.0).astype(jnp.int32).astype(I16)
     acc[...] = jnp.zeros_like(acc)
 
+    span = DSPAN * frames
+    chunk = 2 * HIGH
+    ahead = frames // 8
+    part_rows = frames // 2
+
+    ones = jnp.ones((chunk, 2 * LANES), BF16)
+    zeros = jnp.zeros((chunk, 2 * LANES), BF16)
+
+    def select(begin, size, base, h):
+        target = jnp.full((chunk, 2 * LANES), base + 4 * h, jnp.int32).astype(I16)
+        total = None
+        for k in range(NCHAN // chunk):
+            chosen = jnp.where(dtm[k * chunk : (k + 1) * chunk, :] == target, ones, zeros).astype(F8)
+            term = dot(det[begin : begin + size, k * chunk : (k + 1) * chunk], chosen)
+            total = term if k == 0 else total + term
+        return total
+
+    def shifts(first_row, size):
+        def shift(i, carry):
+            totals = []
+            for j in range(ahead):
+                a = i * ahead + j
+                totals.append([select(first_row, size, 8 * a, h) for h in range(2)])
+            for j in range(ahead):
+                begin = pl.multiple_of(span + first_row - 8 * (i * ahead + j), 8)
+                for h in range(2):
+                    acc[h, pl.ds(begin, size), :] += totals[j][h]
+            return carry
+
+        lax.fori_loop(0, jnp.minimum(me + 1, DSPAN), shift, 0)
+
+        @pl.when(me >= DSPAN)
+        def _():
+            acc[0, first_row : first_row + size, :] += select(first_row, size, span, 0)
+
+    fed_late = (me > 0) & (lax.rem(me, CORES * side) == 0)
+
+    @pl.when(fed_late)
+    def _():
+        shifts(part_rows, part_rows)
+
     @pl.when(me == 1)
     def _():
         pl.semaphore_wait(go_sem, 1)
@@ -262,39 +312,13 @@
 
     hear(0)
 
-    span = DSPAN * frames
-    chunk = 2 * HIGH
-    ahead = frames // 8
-
-    ones = jnp.ones((chunk, 2 * LANES), BF16)
-    zeros = jnp.zeros((chunk, 2 * LANES), BF16)
-
-    def select(base, h):
-        target = jnp.full((chunk, 2 * LANES), base + 4 * h, jnp.int32).astype(I16)
-        total = None
-        for k in range(NCHAN // chunk):
-            chosen = jnp.where(dtm[k * chunk : (k + 1) * chunk, :] == target, ones, zeros)
-            term = dot(det[:, k * chunk : (k + 1) * chunk], chosen)
-            total = term if k == 0 else total + term
-        return total
-
-    def shift(i, carry):
-        totals = []
-        for j in range(ahead):
-            a = i * ahead + j
-            totals.append([select(8 * a, h) for h in range(2)])
-        for j in range(ahead):
-            begin = pl.multiple_of(span - 8 * (i * ahead + j), 8)
-            for h in range(2):
-                acc[h, pl.ds(begin, frames), :] += totals[j][h]
-        return carry
-
-    lax.fori_loop(0, jnp.minimum(me + 1, DSPAN), shift, 0)
-
-    @pl.when(me >= DSPAN)
-    def _():
-        acc[0, 0:frames, :] += select(span, 0)
-
+    @pl.when(fed_late)
+    def _():
+        shifts(0, part_rows)
+
+    @pl.when(jnp.logical_not(fed_late))
+    def _():
+        shifts(0, frames)
 
     hear(1)
 
@@ -473,6 +497,17 @@
             )
         )
     )
+    zscore, stats = pl.pallas_call(
+        hand_on,
+        out_shape=(
+            jax.ShapeDtypeStruct((frames, trials), F32),
+            jax.ShapeDtypeStruct((3, trials), F32),
+        ),
+        in_specs=[pl.BlockSpec(memory_space=pltpu.VMEM)] * 2,
+        out_specs=(pl.BlockSpec(memory_space=pl.ANY),) * 2,
+        scratch_shapes=[dma((2,))],
+        compiler_params=pltpu.CompilerParams(vmem_limit_bytes=1 << 20),
+    )(zscore, stats)
     return zscore.T, stats
 
 

time: 40.8 us -> 38.5 us (0.944)
  local copies, waits for them, and re-layouts: 1.19 us -> 0 us
  Pallas kernels: 38.8 us -> 37.7 us
    pallas_call x1, Pallas kernels: 38.8 us -> 37.1 us  [per_device(): pl.pallas_call(functools.partial(kernel, tm_size, frames, trials), out_sh...]
    unnamed x2 -> x0, local copies, waits for them, and re-layouts: 1.19 us -> none
    pallas_call x0 -> x1, Pallas kernels: none -> 0.63 us  [per_device(): pl.pallas_call(hand_on, out_shape=(jax.ShapeDtypeStruct((frames, trials),...]
where the time goes in v5:
time: 38.5 us; the launch traced here: 38.3 us
  Pallas kernels  37.7 us (98%)
  between operations  0.64 us (2%)
    pallas_call x1, Pallas kernels, per_device(): pl.pallas_call(functools.partial(kernel, tm_size, frames, trials), out_sh...  37.1 us

profile of v5, /device:TPU:513, one launch (start us, length us, event | category | flops | bytes accessed | tf_op | source)
XLA Modules:
  0.0 38.3 jit_solution(7057563703300366637)
XLA Ops:
  0.6 37.1 %shard_map.86 = (f32[32,64]{1,0:T(8,128)S(1)}, f32[3,64]{1,0:T(4,128)S(1)}) custom-call(bf16[2,32,32,128]{3,2,1,0:T(8,128)(2,1)} %bitcast.7, s32[64,2048]{1,0:T(8,128)} %delays.1, s32[1,2048]{1,0:T(1,128)} %bitcast.8, f32[16,32,128]{2,1,0:T(8,128)} %constant.8.clone.coef, bf16[2,256,256]{2,1,0:T(8,128)(2,1)} %constant.9.clone.first, ...), custom_call_target="tpu_custom_call" | custom-call | tf_op jit(solution)/shard_map/pallas_call | solution.py:447
  37.7 0.6 %shard_map.87 = (f32[32,64]{1,0:T(8,128)}, f32[3,64]{1,0:T(4,128)}) custom-call(f32[32,64]{1,0:T(8,128)S(1)} %get-tuple-element.6.zscore, f32[3,64]{1,0:T(4,128)S(1)} %get-tuple-element.7.stats), custom_call_target="tpu_custom_call" | custom-call | tf_op jit(solution)/shard_map/pallas_call | solution.py:500

commit v6 on v5

--- a/solution.py
+++ b/solution.py
@@ -85,7 +85,7 @@
     tm_size, frames, trials,
     volt, delays, mask, coef, first, twist, second,
     zout, stats_out,
-    x, c, b1, tw, b2, dl, mk, wh, wl, det, dt32, dtm, acc, part, parts_in, st_a, st_b,
+    x, c, b1, tw, b2, dl, mk, wh, wl, det, dt32, dtm, sel, acc, part, parts_in, st_a, st_b,
     load_sem, go_sem, all_sem, past_sem, past2_sem, halo_send, halo_recv, part_send, part_recv, pair_send, pair_recv,
     b_send, b_recv,
 ):
@@ -96,6 +96,7 @@
     side = GROUP // CORES
     core = lax.rem(me, CORES)
     place = me // CORES
+    row, col = place // side, lax.rem(place, side)
     chips = rings * side
 
     def signal(sem, target):
@@ -108,14 +109,14 @@
         )
 
     def every_chip(act):
-        def step(k, carry):
-            for j in range(1, SOME + 1):
-                act(lax.rem(place + k * SOME + j, chips))
+        def step(j, carry):
+            for i in range(1, rings + 1):
+                act(lax.rem(row + i, rings) * side + lax.rem(col + 1 + j, side))
             return carry
 
-        lax.fori_loop(0, (chips - 1) // SOME, step, 0)
-        for j in range((chips - 1) // SOME * SOME + 1, chips):
-            act(lax.rem(place + j, chips))
+        lax.fori_loop(0, side - 1, step, 0)
+        for i in range(1, rings):
+            act(lax.rem(row + i, rings) * side + col)
 
     barrier = pltpu.get_barrier_semaphore()
 
@@ -149,13 +150,13 @@
             halo_send.at[k], halo_recv.at[k], me + 1,
         )
 
+    @pl.when(me == 0)
+    def _():
+        pl.semaphore_wait(barrier, last)
+        signal(go_sem, 1)
+
     loads[0].wait()
     loads[1].wait()
-
-    @pl.when(me == 0)
-    def _():
-        pl.semaphore_wait(barrier, last)
-        signal(go_sem, 1)
 
     @pl.when((me > 0) & (me < last))
     def _():
@@ -244,21 +245,25 @@
     ones = jnp.ones((chunk, 2 * LANES), BF16)
     zeros = jnp.zeros((chunk, 2 * LANES), BF16)
 
-    def select(begin, size, base, h):
-        target = jnp.full((chunk, 2 * LANES), base + 4 * h, jnp.int32).astype(I16)
+    def chosen(k, base):
+        target = jnp.full((chunk, 2 * LANES), base, jnp.int32).astype(I16)
+        return jnp.where(dtm[k * chunk : (k + 1) * chunk, :] == target, ones, zeros).astype(F8)
+
+    def select(begin, size, a, h, stored):
         total = None
         for k in range(NCHAN // chunk):
-            chosen = jnp.where(dtm[k * chunk : (k + 1) * chunk, :] == target, ones, zeros).astype(F8)
-            term = dot(det[begin : begin + size, k * chunk : (k + 1) * chunk], chosen)
+            rows = slice(k * chunk, (k + 1) * chunk)
+            weights = sel[2 * a + h, rows, :] if stored else chosen(k, 8 * a + 4 * h)
+            term = dot(det[begin : begin + size, rows], weights)
             total = term if k == 0 else total + term
         return total
 
-    def shifts(first_row, size):
+    def shifts(first_row, size, stored):
         def shift(i, carry):
             totals = []
             for j in range(ahead):
                 a = i * ahead + j
-                totals.append([select(first_row, size, 8 * a, h) for h in range(2)])
+                totals.append([select(first_row, size, a, h, stored) for h in range(2)])
             for j in range(ahead):
                 begin = pl.multiple_of(span + first_row - 8 * (i * ahead + j), 8)
                 for h in range(2):
@@ -269,25 +274,38 @@
 
         @pl.when(me >= DSPAN)
         def _():
-            acc[0, first_row : first_row + size, :] += select(first_row, size, span, 0)
-
-    fed_late = (me > 0) & (lax.rem(me, CORES * side) == 0)
+            acc[0, first_row : first_row + size, :] += select(first_row, size, span // 8, 0, stored)
+
+    fed_late = (me == 1) | ((me > 1) & (lax.rem(me, CORES * side) == 0))
 
     @pl.when(fed_late)
     def _():
-        shifts(part_rows, part_rows)
+        def keep(q, carry):
+            for k in range(NCHAN // chunk):
+                sel[q, k * chunk : (k + 1) * chunk, :] = chosen(k, 4 * q)
+            return carry
+
+        lax.fori_loop(0, span // 4 + 1, keep, 0)
+        shifts(part_rows, part_rows, True)
 
     @pl.when(me == 1)
     def _():
         pl.semaphore_wait(go_sem, 1)
         signal(past_sem, 2)
-        signal(go_sem, DSPAN)
+        signal(go_sem, 2)
+        signal(go_sem, 3)
 
     for k in range(4):
 
         @pl.when(me > 0)
         def _():
             halo(k).wait_recv()
+
+        if k == 0:
+
+            @pl.when((me > 1) & (me < last))
+            def _():
+                signal(past_sem, me + 1)
 
         def early_half(block, carry):
             weigh(block, k)
@@ -295,14 +313,10 @@
 
         lax.fori_loop(0, 2, early_half, 0)
 
-    @pl.when((me > 1) & (me < last))
-    def _():
-        signal(past_sem, me + 1)
-
     transform(0)
 
-    def hear(parity):
-        @pl.when((me > 1) & (core == parity))
+    def hear(now):
+        @pl.when((me > 1) & now)
         def _():
             pl.semaphore_wait(past_sem, 1)
 
@@ -310,17 +324,18 @@
             def _():
                 signal(past2_sem, me + 1)
 
-    hear(0)
+    top = lax.rem(place, side) == 0
+    hear(((core == 0) & (me > 2)) | ((core == 1) & jnp.logical_not(top)))
 
     @pl.when(fed_late)
     def _():
-        shifts(0, part_rows)
+        shifts(0, part_rows, True)
 
     @pl.when(jnp.logical_not(fed_late))
     def _():
-        shifts(0, frames)
-
-    hear(1)
+        shifts(0, frames, False)
+
+    hear(((core == 1) & top) | (me == 2))
 
     even, odd = None, None
     rows_out = span + frames
@@ -352,20 +367,19 @@
         def _():
             parts_in[k - 1] = jnp.zeros((frames, LANES), F32)
 
-    @pl.when(me == DSPAN)
+    @pl.when((me == 2) | (me == 3))
     def _():
         pl.semaphore_wait(go_sem, 1)
 
         def tell(k, carry):
-            for j in range(SOME):
-                signal(all_sem, DSPAN + 1 + k * SOME + j)
+            for j in range(1, SOME + 1):
+                signal(all_sem, me + 2 * (k * SOME + j))
             return carry
 
-        others = tm_size - 1 - DSPAN
-        signal(all_sem, 2)
+        others = (tm_size - 4) // 2
         lax.fori_loop(0, others // SOME, tell, 0)
-        for j in range(others // SOME * SOME, others):
-            signal(all_sem, DSPAN + 1 + j)
+        for j in range(others // SOME * SOME + 1, others + 1):
+            signal(all_sem, me + 2 * j)
 
     for k in range(1, DSPAN + 1):
 
@@ -396,7 +410,7 @@
     st_a[0] = pack(mean, second_sum, jnp.max(series, axis=0, keepdims=True))
     part[span:, :] = series
 
-    @pl.when((me > 1) & (me != DSPAN))
+    @pl.when(me > 3)
     def _():
         pl.semaphore_wait(all_sem, 1)
 
@@ -465,6 +479,7 @@
             vmem((frames, NCHAN), BF16),
             vmem((NCHAN, LANES), F32),
             vmem((NCHAN, 2 * LANES), I16),
+            vmem((span // 4 + 1, NCHAN, 2 * LANES), F8),
             vmem((2, span + frames + 8, 2 * LANES), F32),
             vmem((span + frames, LANES), F32),
             vmem((DSPAN, frames, LANES), F32),

time: 38.5 us -> 38 us (0.987)
  the two profiles are of different devices: /device:TPU:513 before, /device:TPU:640 now
where the time goes in v6:
time: 38 us; the launch traced here: 37.9 us
  Pallas kernels  37.3 us (98%)
  between operations  0.64 us (2%)
    pallas_call x1, Pallas kernels, per_device(): pl.pallas_call(functools.partial(kernel, tm_size, frames, trials), out_sh...  36.6 us

profile of v6, /device:TPU:640, one launch (start us, length us, event | category | flops | bytes accessed | tf_op | source)
XLA Modules:
  0.0 37.9 jit_solution(18237487460116973089)
XLA Ops:
  0.6 36.6 %shard_map.86 = (f32[32,64]{1,0:T(8,128)S(1)}, f32[3,64]{1,0:T(4,128)S(1)}) custom-call(bf16[2,32,32,128]{3,2,1,0:T(8,128)(2,1)} %bitcast.7, s32[64,2048]{1,0:T(8,128)} %delays.1, s32[1,2048]{1,0:T(1,128)} %bitcast.8, f32[16,32,128]{2,1,0:T(8,128)} %constant.8.clone.coef, bf16[2,256,256]{2,1,0:T(8,128)(2,1)} %constant.9.clone.first, ...), custom_call_target="tpu_custom_call" | custom-call | tf_op jit(solution)/shard_map/pallas_call | solution.py:461
  37.3 0.6 %shard_map.87 = (f32[32,64]{1,0:T(8,128)}, f32[3,64]{1,0:T(4,128)}) custom-call(f32[32,64]{1,0:T(8,128)S(1)} %get-tuple-element.6.zscore, f32[3,64]{1,0:T(4,128)S(1)} %get-tuple-element.7.stats), custom_call_target="tpu_custom_call" | custom-call | tf_op jit(solution)/shard_map/pallas_call | solution.py:515

commit v7 on v6

--- a/solution.py
+++ b/solution.py
@@ -21,7 +21,7 @@
 MESH = pl.DeviceIdType.MESH
 F32 = jnp.float32
 BF16 = jnp.bfloat16
-I16 = jnp.int16
+I8 = jnp.int8
 F8 = jnp.float8_e4m3fn
 
 
@@ -85,7 +85,7 @@
     tm_size, frames, trials,
     volt, delays, mask, coef, first, twist, second,
     zout, stats_out,
-    x, c, b1, tw, b2, dl, mk, wh, wl, det, dt32, dtm, sel, acc, part, parts_in, st_a, st_b,
+    x, c, b1, tw, b2, dl, mk, wh, wl, det, dt32, dtm, acc, part, parts_in, st_a, st_b,
     load_sem, go_sem, all_sem, past_sem, past2_sem, halo_send, halo_recv, part_send, part_recv, pair_send, pair_recv,
     b_send, b_recv,
 ):
@@ -171,7 +171,7 @@
     def _():
         x[:, :hist] = jnp.zeros((2, hist, 2 * LOW, HIGH), BF16)
 
-    for load in loads[2:]:
+    for load in loads[2:5]:
         load.wait()
 
     def weigh(block, k):
@@ -221,7 +221,12 @@
         return carry
 
     lax.fori_loop(0, 4, late_half, 0)
+    for load in loads[5:8]:
+        load.wait()
     transform(1)
+
+    for load in loads[8:]:
+        load.wait()
 
     used = jnp.where(mk[...] > 0, dl[...], -1).astype(F32).astype(BF16)
     lane = lax.broadcasted_iota(jnp.int32, (trials, LANES), 1)
@@ -233,60 +238,9 @@
     offset = (lane_k // trials).astype(F32)
     for k in range(LOW):
         rows = dt32[pl.ds(k, HIGH, stride=LOW), :] - offset
-        dtm[k * HIGH : (k + 1) * HIGH, :LANES] = rows.astype(jnp.int32).astype(I16)
-        dtm[k * HIGH : (k + 1) * HIGH, LANES:] = (rows - 2.0).astype(jnp.int32).astype(I16)
+        dtm[k * HIGH : (k + 1) * HIGH, :LANES] = rows.astype(jnp.int32).astype(I8)
+        dtm[k * HIGH : (k + 1) * HIGH, LANES:] = (rows - 2.0).astype(jnp.int32).astype(I8)
     acc[...] = jnp.zeros_like(acc)
-
-    span = DSPAN * frames
-    chunk = 2 * HIGH
-    ahead = frames // 8
-    part_rows = frames // 2
-
-    ones = jnp.ones((chunk, 2 * LANES), BF16)
-    zeros = jnp.zeros((chunk, 2 * LANES), BF16)
-
-    def chosen(k, base):
-        target = jnp.full((chunk, 2 * LANES), base, jnp.int32).astype(I16)
-        return jnp.where(dtm[k * chunk : (k + 1) * chunk, :] == target, ones, zeros).astype(F8)
-
-    def select(begin, size, a, h, stored):
-        total = None
-        for k in range(NCHAN // chunk):
-            rows = slice(k * chunk, (k + 1) * chunk)
-            weights = sel[2 * a + h, rows, :] if stored else chosen(k, 8 * a + 4 * h)
-            term = dot(det[begin : begin + size, rows], weights)
-            total = term if k == 0 else total + term
-        return total
-
-    def shifts(first_row, size, stored):
-        def shift(i, carry):
-            totals = []
-            for j in range(ahead):
-                a = i * ahead + j
-                totals.append([select(first_row, size, a, h, stored) for h in range(2)])
-            for j in range(ahead):
-                begin = pl.multiple_of(span + first_row - 8 * (i * ahead + j), 8)
-                for h in range(2):
-                    acc[h, pl.ds(begin, size), :] += totals[j][h]
-            return carry
-
-        lax.fori_loop(0, jnp.minimum(me + 1, DSPAN), shift, 0)
-
-        @pl.when(me >= DSPAN)
-        def _():
-            acc[0, first_row : first_row + size, :] += select(first_row, size, span // 8, 0, stored)
-
-    fed_late = (me == 1) | ((me > 1) & (lax.rem(me, CORES * side) == 0))
-
-    @pl.when(fed_late)
-    def _():
-        def keep(q, carry):
-            for k in range(NCHAN // chunk):
-                sel[q, k * chunk : (k + 1) * chunk, :] = chosen(k, 4 * q)
-            return carry
-
-        lax.fori_loop(0, span // 4 + 1, keep, 0)
-        shifts(part_rows, part_rows, True)
 
     @pl.when(me == 1)
     def _():
@@ -327,13 +281,35 @@
     top = lax.rem(place, side) == 0
     hear(((core == 0) & (me > 2)) | ((core == 1) & jnp.logical_not(top)))
 
-    @pl.when(fed_late)
-    def _():
-        shifts(0, part_rows, True)
-
-    @pl.when(jnp.logical_not(fed_late))
-    def _():
-        shifts(0, frames, False)
+    span = DSPAN * frames
+    chunk = 2 * HIGH
+    ahead = frames // 8
+
+    ones = jnp.ones((chunk, 2 * LANES), F8)
+    zeros = jnp.zeros((chunk, 2 * LANES), F8)
+
+    def select(base):
+        target = jnp.full((chunk, 2 * LANES), base, jnp.int32).astype(I8)
+        total = None
+        for k in range(NCHAN // chunk):
+            rows = slice(k * chunk, (k + 1) * chunk)
+            term = dot(det[:, rows], jnp.where(dtm[rows, :] == target, ones, zeros))
+            total = term if k == 0 else total + term
+        return total
+
+    def shift(i, carry):
+        totals = [[select(8 * (i * ahead + j) + 4 * h) for h in range(2)] for j in range(ahead)]
+        for j in range(ahead):
+            begin = pl.multiple_of(span - 8 * (i * ahead + j), 8)
+            for h in range(2):
+                acc[h, pl.ds(begin, frames), :] += totals[j][h]
+        return carry
+
+    lax.fori_loop(0, jnp.minimum(me + 1, DSPAN), shift, 0)
+
+    @pl.when(me >= DSPAN)
+    def _():
+        acc[0, 0:frames, :] += select(span)
 
     hear(((core == 1) & top) | (me == 2))
 
@@ -410,14 +386,14 @@
     st_a[0] = pack(mean, second_sum, jnp.max(series, axis=0, keepdims=True))
     part[span:, :] = series
 
-    @pl.when(me > 3)
-    def _():
-        pl.semaphore_wait(all_sem, 1)
-
     pair = send(st_a.at[0], st_a.at[1], pair_send, pair_recv, me + 1 - 2 * core)
     pair.start()
     pair.wait_recv()
     st_b[place] = pack(*merge(st_a, CORES, float(frames)))
+
+    @pl.when(me > 3)
+    def _():
+        pl.semaphore_wait(all_sem, 1)
 
     def chip_copy(chip):
         return send(st_b.at[place], st_b.at[place], b_send, b_recv, chip * CORES + core)
@@ -478,8 +454,7 @@
             vmem((frames // BLOCK, side, 2 * LANES), BF16),
             vmem((frames, NCHAN), BF16),
             vmem((NCHAN, LANES), F32),
-            vmem((NCHAN, 2 * LANES), I16),
-            vmem((span // 4 + 1, NCHAN, 2 * LANES), F8),
+            vmem((NCHAN, 2 * LANES), I8),
             vmem((2, span + frames + 8, 2 * LANES), F32),
             vmem((span + frames, LANES), F32),
             vmem((DSPAN, frames, LANES), F32),

time: 38 us -> 36.9 us (0.971)
  the two profiles are of different devices: /device:TPU:640 before, /device:TPU:513 now
where the time goes in v7:
time: 36.9 us; the launch traced here: 36.5 us
  Pallas kernels  35.9 us (97%)
  between operations  0.64 us (2%)
    pallas_call x1, Pallas kernels, per_device(): pl.pallas_call(functools.partial(kernel, tm_size, frames, trials), out_sh...  35.3 us

profile of v7, /device:TPU:513, one launch (start us, length us, event | category | flops | bytes accessed | tf_op | source)
XLA Modules:
  0.0 36.5 jit_solution(6850163892523746586)
XLA Ops:
  0.6 35.3 %shard_map.86 = (f32[32,64]{1,0:T(8,128)S(1)}, f32[3,64]{1,0:T(4,128)S(1)}) custom-call(bf16[2,32,32,128]{3,2,1,0:T(8,128)(2,1)} %bitcast.7, s32[64,2048]{1,0:T(8,128)} %delays.1, s32[1,2048]{1,0:T(1,128)} %bitcast.8, f32[16,32,128]{2,1,0:T(8,128)} %constant.8.clone.coef, bf16[2,256,256]{2,1,0:T(8,128)(2,1)} %constant.9.clone.first, ...), custom_call_target="tpu_custom_call" | custom-call | tf_op jit(solution)/shard_map/pallas_call | solution.py:437
  35.9 0.6 %shard_map.87 = (f32[32,64]{1,0:T(8,128)}, f32[3,64]{1,0:T(4,128)}) custom-call(f32[32,64]{1,0:T(8,128)S(1)} %get-tuple-element.6.zscore, f32[3,64]{1,0:T(4,128)S(1)} %get-tuple-element.7.stats), custom_call_target="tpu_custom_call" | custom-call | tf_op jit(solution)/shard_map/pallas_call | solution.py:490
